TPU v7x, 32 devices: a 4x4x1 block of a 4x4x8 slice. The times are simulated.
32 devices in a mesh: data: 1 (over z), col: 4 (over y), row: 8 (over x, core).
Axes of the slice: x: 4, y: 4, z: 1, core: 2. Of those that a mesh axis runs over, the one named last changes fastest.
The devices are a block of a 4x4x8 slice.
Arguments:
- seq_in: bfloat16 [16, 8, 2816], P(None, 'data', 'row')
- w_x1: bfloat16 [2816, 11264], P('row', 'col')
- w_h1: bfloat16 [2816, 11264], P('row', 'col')
- w_x2: bfloat16 [2816, 11264], P('row', 'col')
- w_h2: bfloat16 [2816, 11264], P('row', 'col')
- bias_1: float32 [11264], P('col')
- bias_2: float32 [11264], P('col')
- h_init: float32 [2, 8, 2816], P(None, 'data', 'row')
- c_init: float32 [2, 8, 2816], P(None, 'data', 'row')
- g_out: bfloat16 [16, 8, 2816], P(None, 'data', 'col')
Outputs:
- output 1: float32 [2816, 11264], P(('data', 'row'), 'col')
- output 2: float32 [2816, 11264], P(('data', 'row'), 'col')
- output 3: float32 [2816, 11264], P(('data', 'row'), 'col')
- output 4: float32 [2816, 11264], P(('data', 'row'), 'col')
- output 5: float32 [11264], P(('data', 'col'))
- output 6: float32 [11264], P(('data', 'col'))
All inputs are finite; a program needn't handle non-finite values.
Results may differ from a plain program's by a relative error of at most 0.0062514.
Values are sent between devices in bfloat16 or wider.
A program may use at most 768 MiB of HBM per device.

v0:
```python
import jax
import jax.numpy as jnp
from jax import lax
from jax.sharding import PartitionSpec as P


def gate_acts(pre_act):
    grouped = pre_act.reshape(pre_act.shape[:-1] + (pre_act.shape[-1] // 4, 4))
    squashed = jax.nn.sigmoid(grouped)
    return jnp.stack([squashed[..., 0], squashed[..., 1], jnp.tanh(grouped[..., 2]), squashed[..., 3]], axis=-1)


def cell_grad(dh_tot, dc_next, gate_vals, c_prev, tanh_c):
    in_g = gate_vals[..., 0]
    fgt_g = gate_vals[..., 1]
    cand_g = gate_vals[..., 2]
    out_g = gate_vals[..., 3]
    dc_tot = dc_next + dh_tot * out_g * (1.0 - tanh_c * tanh_c)
    stacked = jnp.stack([
        dc_tot * cand_g * in_g * (1.0 - in_g),
        dc_tot * c_prev * fgt_g * (1.0 - fgt_g),
        dc_tot * in_g * (1.0 - cand_g * cand_g),
        dh_tot * tanh_c * out_g * (1.0 - out_g)], axis=-1)
    return stacked.reshape(stacked.shape[:-2] + (4 * stacked.shape[-2],)), dc_tot * fgt_g


def layer_forward(in_rows, w_in, w_rec, bias_cols, h_start, c_start, row_idx):
    row_width = w_rec.shape[0]
    projected = lax.psum(jnp.einsum('tbk,kn->tbn', in_rows, w_in, preferred_element_type=jnp.float32), 'row') + bias_cols

    def step_fn(carried, u_t):
        h_rows, c_prev = carried
        pre_act = u_t + lax.psum(jnp.dot(h_rows, w_rec, preferred_element_type=jnp.float32), 'row')
        gate_vals = gate_acts(pre_act)
        c_new = gate_vals[..., 1] * c_prev + gate_vals[..., 0] * gate_vals[..., 2]
        tanh_c = jnp.tanh(c_new)
        h_cols = (gate_vals[..., 3] * tanh_c).astype(jnp.bfloat16)
        h_full = lax.all_gather(h_cols, 'col', axis=1, tiled=True)
        h_next = lax.dynamic_slice_in_dim(h_full, row_idx * row_width, row_width, axis=1)
        return (h_next, c_new), (h_next, c_prev, tanh_c, gate_vals)

    return lax.scan(step_fn, (h_start, c_start), projected)[1]


def layer_backward(dh_seq, gate_seq, c_prev_seq, tanh_seq, w_rec, col_idx):
    n_batch = dh_seq.shape[1]
    col_width = dh_seq.shape[2]

    def step_fn(carried, inputs_t):
        dh_next, dc_next, bias_acc = carried
        dh_out, gate_vals, c_prev, tanh_c = inputs_t
        d_pre, dc_prev = cell_grad(dh_out + dh_next, dc_next, gate_vals, c_prev, tanh_c)
        d_pre_bf = d_pre.astype(jnp.bfloat16)
        row_part = lax.dot_general(d_pre_bf, w_rec, (((1,), (1,)), ((), ())), preferred_element_type=jnp.float32)
        dh_full = lax.all_gather(lax.psum(row_part, 'col'), 'row', axis=1, tiled=True)
        dh_rec = lax.dynamic_slice_in_dim(dh_full, col_idx * col_width, col_width, axis=1)
        return (dh_rec, dc_prev, bias_acc + jnp.sum(d_pre, axis=0)), d_pre_bf

    zero_carry = (jnp.zeros((n_batch, col_width), jnp.float32), jnp.zeros((n_batch, col_width), jnp.float32), jnp.zeros((4 * col_width,), jnp.float32))
    final_carry, dz_seq = lax.scan(step_fn, zero_carry, (dh_seq, gate_seq, c_prev_seq, tanh_seq), reverse=True)
    return dz_seq, final_carry[2]


def solution(mesh):
    seq_spec = P(None, 'data', 'row')
    w_spec = P('row', 'col')
    bias_spec = P('col')
    g_spec = P(None, 'data', 'col')
    grad_spec = P(('data', 'row'), 'col')
    gbias_spec = P(('data', 'col'))

    def local_grads(seq_in, w_x1, w_h1, w_x2, w_h2, bias_1, bias_2, h_init, c_init, g_out):
        row_idx = lax.axis_index('row')
        col_idx = lax.axis_index('col')
        col_width = w_x1.shape[1] // 4
        h_first = h_init.astype(jnp.bfloat16)
        c_full = lax.all_gather(c_init, 'row', axis=2, tiled=True)
        c_first = lax.dynamic_slice_in_dim(c_full, col_idx * col_width, col_width, axis=2)
        h1_rows, c1_prev, tanh_c1, gates_l1 = layer_forward(seq_in, w_x1, w_h1, bias_1, h_first[0], c_first[0], row_idx)
        h2_rows, c2_prev, tanh_c2, gates_l2 = layer_forward(h1_rows, w_x2, w_h2, bias_2, h_first[1], c_first[1], row_idx)
        dz_l2, grad_b2 = layer_backward(g_out, gates_l2, c2_prev, tanh_c2, w_h2, col_idx)
        grad_wh2 = jnp.einsum('tbk,tbn->kn', jnp.concatenate([h_first[1:2], h2_rows[:-1]], axis=0), dz_l2, preferred_element_type=jnp.float32)
        grad_wx2 = jnp.einsum('tbk,tbn->kn', h1_rows, dz_l2, preferred_element_type=jnp.float32)
        dh_part = jnp.einsum('tbn,kn->tbk', dz_l2, w_x2, preferred_element_type=jnp.float32)
        dh_full = lax.all_gather(lax.psum(dh_part, 'col'), 'row', axis=2, tiled=True)
        dh_l1 = lax.dynamic_slice_in_dim(dh_full, col_idx * col_width, col_width, axis=2)
        dz_l1, grad_b1 = layer_backward(dh_l1, gates_l1, c1_prev, tanh_c1, w_h1, col_idx)
        grad_wh1 = jnp.einsum('tbk,tbn->kn', jnp.concatenate([h_first[0:1], h1_rows[:-1]], axis=0), dz_l1, preferred_element_type=jnp.float32)
        grad_wx1 = jnp.einsum('tbk,tbn->kn', seq_in, dz_l1, preferred_element_type=jnp.float32)
        return grad_wx1, grad_wh1, grad_wx2, grad_wh2, grad_b1, grad_b2

    return jax.shard_map(local_grads, mesh=mesh,
                         in_specs=(seq_spec, w_spec, w_spec, w_spec, w_spec, bias_spec, bias_spec, seq_spec, seq_spec, g_spec),
                         out_specs=(grad_spec, grad_spec, grad_spec, grad_spec, gbias_spec, gbias_spec),
                         check_vma=False)
```

profile of v0, /device:TPU:97, one launch (start us, length us, event | category | flops | bytes accessed | tf_op | source)
XLA Modules:
  0.0 3956.2 jit_solution(7604846470266415949)
XLA Ops:
  12.2 31.3 all_gather.34
  44.9 30.6 all-reduce.6.cloned.1.call-done
  81.6 1144.9 %while.86 = (s32[]{:T(128)}, bf16[8,352]{1,0:T(8,128)(2,1)S(1)}, f32[8,704]{1,0:T(8,128)S(1)}, bf16[16,8,352]{2,1,0:T(8,128)(2,1)}, f32[16,8,704]{2,1,0:T(8,128)...) while((s32[]{:T(128)}, bf16[8,352]{1,0:T(8,128)(2,1)S(1)}, ...), condition=%wide.region_3.4_spmd, body=%wide.region_1.3_spmd.sunk | while | flops 16045570 | bytes 4276913 | solution.py:42
  84.2 54.6 %all-reduce.12.cloned.1.call-done = f32[8,2816]{1,0:T(8,128)} async-done(((f32[8,2816]{1,0:T(8,128)}), f32[8,2816]{1,0:T(8,128)}) %all-reduce.12.cloned.1.call-update) | async-done | bytes 90128 | tf_op jit(solution)/shard_map/while/body/eval_jaxpr/psum | solution.py:33
  155.2 55.3 %all-reduce.12.cloned.1.call-done = f32[8,2816]{1,0:T(8,128)} async-done(((f32[8,2816]{1,0:T(8,128)}), f32[8,2816]{1,0:T(8,128)}) %all-reduce.12.cloned.1.call-update) | async-done | bytes 90128 | tf_op jit(solution)/shard_map/while/body/eval_jaxpr/psum | solution.py:33
  227.0 55.0 %all-reduce.12.cloned.1.call-done = f32[8,2816]{1,0:T(8,128)} async-done(((f32[8,2816]{1,0:T(8,128)}), f32[8,2816]{1,0:T(8,128)}) %all-reduce.12.cloned.1.call-update) | async-done | bytes 90128 | tf_op jit(solution)/shard_map/while/body/eval_jaxpr/psum | solution.py:33
  298.5 55.0 %all-reduce.12.cloned.1.call-done = f32[8,2816]{1,0:T(8,128)} async-done(((f32[8,2816]{1,0:T(8,128)}), f32[8,2816]{1,0:T(8,128)}) %all-reduce.12.cloned.1.call-update) | async-done | bytes 90128 | tf_op jit(solution)/shard_map/while/body/eval_jaxpr/psum | solution.py:33
  370.0 55.0 %all-reduce.12.cloned.1.call-done = f32[8,2816]{1,0:T(8,128)} async-done(((f32[8,2816]{1,0:T(8,128)}), f32[8,2816]{1,0:T(8,128)}) %all-reduce.12.cloned.1.call-update) | async-done | bytes 90128 | tf_op jit(solution)/shard_map/while/body/eval_jaxpr/psum | solution.py:33
  441.4 55.4 %all-reduce.12.cloned.1.call-done = f32[8,2816]{1,0:T(8,128)} async-done(((f32[8,2816]{1,0:T(8,128)}), f32[8,2816]{1,0:T(8,128)}) %all-reduce.12.cloned.1.call-update) | async-done | bytes 90128 | tf_op jit(solution)/shard_map/while/body/eval_jaxpr/psum | solution.py:33
  513.2 55.4 %all-reduce.12.cloned.1.call-done = f32[8,2816]{1,0:T(8,128)} async-done(((f32[8,2816]{1,0:T(8,128)}), f32[8,2816]{1,0:T(8,128)}) %all-reduce.12.cloned.1.call-update) | async-done | bytes 90128 | tf_op jit(solution)/shard_map/while/body/eval_jaxpr/psum | solution.py:33
  585.0 55.3 %all-reduce.12.cloned.1.call-done = f32[8,2816]{1,0:T(8,128)} async-done(((f32[8,2816]{1,0:T(8,128)}), f32[8,2816]{1,0:T(8,128)}) %all-reduce.12.cloned.1.call-update) | async-done | bytes 90128 | tf_op jit(solution)/shard_map/while/body/eval_jaxpr/psum | solution.py:33
  656.7 55.0 %all-reduce.12.cloned.1.call-done = f32[8,2816]{1,0:T(8,128)} async-done(((f32[8,2816]{1,0:T(8,128)}), f32[8,2816]{1,0:T(8,128)}) %all-reduce.12.cloned.1.call-update) | async-done | bytes 90128 | tf_op jit(solution)/shard_map/while/body/eval_jaxpr/psum | solution.py:33
  728.2 55.3 %all-reduce.12.cloned.1.call-done = f32[8,2816]{1,0:T(8,128)} async-done(((f32[8,2816]{1,0:T(8,128)}), f32[8,2816]{1,0:T(8,128)}) %all-reduce.12.cloned.1.call-update) | async-done | bytes 90128 | tf_op jit(solution)/shard_map/while/body/eval_jaxpr/psum | solution.py:33
  800.0 55.0 %all-reduce.12.cloned.1.call-done = f32[8,2816]{1,0:T(8,128)} async-done(((f32[8,2816]{1,0:T(8,128)}), f32[8,2816]{1,0:T(8,128)}) %all-reduce.12.cloned.1.call-update) | async-done | bytes 90128 | tf_op jit(solution)/shard_map/while/body/eval_jaxpr/psum | solution.py:33
  871.5 55.4 %all-reduce.12.cloned.1.call-done = f32[8,2816]{1,0:T(8,128)} async-done(((f32[8,2816]{1,0:T(8,128)}), f32[8,2816]{1,0:T(8,128)}) %all-reduce.12.cloned.1.call-update) | async-done | bytes 90128 | tf_op jit(solution)/shard_map/while/body/eval_jaxpr/psum | solution.py:33
  943.3 55.0 %all-reduce.12.cloned.1.call-done = f32[8,2816]{1,0:T(8,128)} async-done(((f32[8,2816]{1,0:T(8,128)}), f32[8,2816]{1,0:T(8,128)}) %all-reduce.12.cloned.1.call-update) | async-done | bytes 90128 | tf_op jit(solution)/shard_map/while/body/eval_jaxpr/psum | solution.py:33
  1014.7 55.0 %all-reduce.12.cloned.1.call-done = f32[8,2816]{1,0:T(8,128)} async-done(((f32[8,2816]{1,0:T(8,128)}), f32[8,2816]{1,0:T(8,128)}) %all-reduce.12.cloned.1.call-update) | async-done | bytes 90128 | tf_op jit(solution)/shard_map/while/body/eval_jaxpr/psum | solution.py:33
  1086.2 55.0 %all-reduce.12.cloned.1.call-done = f32[8,2816]{1,0:T(8,128)} async-done(((f32[8,2816]{1,0:T(8,128)}), f32[8,2816]{1,0:T(8,128)}) %all-reduce.12.cloned.1.call-update) | async-done | bytes 90128 | tf_op jit(solution)/shard_map/while/body/eval_jaxpr/psum | solution.py:33
  1157.6 55.0 %all-reduce.12.cloned.1.call-done = f32[8,2816]{1,0:T(8,128)} async-done(((f32[8,2816]{1,0:T(8,128)}), f32[8,2816]{1,0:T(8,128)}) %all-reduce.12.cloned.1.call-update) | async-done | bytes 90128 | tf_op jit(solution)/shard_map/while/body/eval_jaxpr/psum | solution.py:33
  1229.3 59.3 %all-reduce.8.cloned.1.call-done = f32[16,8,2816]{2,1,0:T(8,128)} async-done(((f32[16,8,2816]{2,1,0:T(8,128)}), f32[16,8,2816]{2,1,0:T(8,128)}) %all-reduce.8.cloned.1.call-update) | async-done | bytes 1441808 | tf_op jit(solution)/shard_map/psum | solution.py:29
  1294.7 1136.6 %while.87 = (s32[]{:T(128)}, bf16[8,352]{1,0:T(8,128)(2,1)S(1)}, f32[8,704]{1,0:T(8,128)S(1)}, bf16[16,8,352]{2,1,0:T(8,128)(2,1)}, f32[16,8,704]{2,1,0:T(8,128)...) while((s32[]{:T(128)}, bf16[8,352]{1,0:T(8,128)(2,1)S(1)}, ...), condition=%wide.region_7.8_spmd, body=%wide.region_5.7_spmd.sunk | while | flops 16045570 | bytes 4276913 | solution.py:42
  1297.3 54.0 %all-reduce.14.cloned.1.call-done = f32[8,2816]{1,0:T(8,128)} async-done(((f32[8,2816]{1,0:T(8,128)}), f32[8,2816]{1,0:T(8,128)}) %all-reduce.14.cloned.1.call-update) | async-done | bytes 90128 | tf_op jit(solution)/shard_map/while/body/eval_jaxpr/psum | solution.py:33
  1367.8 54.5 %all-reduce.14.cloned.1.call-done = f32[8,2816]{1,0:T(8,128)} async-done(((f32[8,2816]{1,0:T(8,128)}), f32[8,2816]{1,0:T(8,128)}) %all-reduce.14.cloned.1.call-update) | async-done | bytes 90128 | tf_op jit(solution)/shard_map/while/body/eval_jaxpr/psum | solution.py:33
  1438.7 54.8 %all-reduce.14.cloned.1.call-done = f32[8,2816]{1,0:T(8,128)} async-done(((f32[8,2816]{1,0:T(8,128)}), f32[8,2816]{1,0:T(8,128)}) %all-reduce.14.cloned.1.call-update) | async-done | bytes 90128 | tf_op jit(solution)/shard_map/while/body/eval_jaxpr/psum | solution.py:33
  1509.9 54.8 %all-reduce.14.cloned.1.call-done = f32[8,2816]{1,0:T(8,128)} async-done(((f32[8,2816]{1,0:T(8,128)}), f32[8,2816]{1,0:T(8,128)}) %all-reduce.14.cloned.1.call-update) | async-done | bytes 90128 | tf_op jit(solution)/shard_map/while/body/eval_jaxpr/psum | solution.py:33
  1581.1 54.8 %all-reduce.14.cloned.1.call-done = f32[8,2816]{1,0:T(8,128)} async-done(((f32[8,2816]{1,0:T(8,128)}), f32[8,2816]{1,0:T(8,128)}) %all-reduce.14.cloned.1.call-update) | async-done | bytes 90128 | tf_op jit(solution)/shard_map/while/body/eval_jaxpr/psum | solution.py:33
  1652.3 54.5 %all-reduce.14.cloned.1.call-done = f32[8,2816]{1,0:T(8,128)} async-done(((f32[8,2816]{1,0:T(8,128)}), f32[8,2816]{1,0:T(8,128)}) %all-reduce.14.cloned.1.call-update) | async-done | bytes 90128 | tf_op jit(solution)/shard_map/while/body/eval_jaxpr/psum | solution.py:33
  1723.2 54.8 %all-reduce.14.cloned.1.call-done = f32[8,2816]{1,0:T(8,128)} async-done(((f32[8,2816]{1,0:T(8,128)}), f32[8,2816]{1,0:T(8,128)}) %all-reduce.14.cloned.1.call-update) | async-done | bytes 90128 | tf_op jit(solution)/shard_map/while/body/eval_jaxpr/psum | solution.py:33
  1794.4 54.5 %all-reduce.14.cloned.1.call-done = f32[8,2816]{1,0:T(8,128)} async-done(((f32[8,2816]{1,0:T(8,128)}), f32[8,2816]{1,0:T(8,128)}) %all-reduce.14.cloned.1.call-update) | async-done | bytes 90128 | tf_op jit(solution)/shard_map/while/body/eval_jaxpr/psum | solution.py:33
  1865.3 54.5 %all-reduce.14.cloned.1.call-done = f32[8,2816]{1,0:T(8,128)} async-done(((f32[8,2816]{1,0:T(8,128)}), f32[8,2816]{1,0:T(8,128)}) %all-reduce.14.cloned.1.call-update) | async-done | bytes 90128 | tf_op jit(solution)/shard_map/while/body/eval_jaxpr/psum | solution.py:33
  1936.2 54.8 %all-reduce.14.cloned.1.call-done = f32[8,2816]{1,0:T(8,128)} async-done(((f32[8,2816]{1,0:T(8,128)}), f32[8,2816]{1,0:T(8,128)}) %all-reduce.14.cloned.1.call-update) | async-done | bytes 90128 | tf_op jit(solution)/shard_map/while/body/eval_jaxpr/psum | solution.py:33
  2007.4 54.8 %all-reduce.14.cloned.1.call-done = f32[8,2816]{1,0:T(8,128)} async-done(((f32[8,2816]{1,0:T(8,128)}), f32[8,2816]{1,0:T(8,128)}) %all-reduce.14.cloned.1.call-update) | async-done | bytes 90128 | tf_op jit(solution)/shard_map/while/body/eval_jaxpr/psum | solution.py:33
  2078.6 54.5 %all-reduce.14.cloned.1.call-done = f32[8,2816]{1,0:T(8,128)} async-done(((f32[8,2816]{1,0:T(8,128)}), f32[8,2816]{1,0:T(8,128)}) %all-reduce.14.cloned.1.call-update) | async-done | bytes 90128 | tf_op jit(solution)/shard_map/while/body/eval_jaxpr/psum | solution.py:33
  2149.5 54.8 %all-reduce.14.cloned.1.call-done = f32[8,2816]{1,0:T(8,128)} async-done(((f32[8,2816]{1,0:T(8,128)}), f32[8,2816]{1,0:T(8,128)}) %all-reduce.14.cloned.1.call-update) | async-done | bytes 90128 | tf_op jit(solution)/shard_map/while/body/eval_jaxpr/psum | solution.py:33
  2220.7 54.8 %all-reduce.14.cloned.1.call-done = f32[8,2816]{1,0:T(8,128)} async-done(((f32[8,2816]{1,0:T(8,128)}), f32[8,2816]{1,0:T(8,128)}) %all-reduce.14.cloned.1.call-update) | async-done | bytes 90128 | tf_op jit(solution)/shard_map/while/body/eval_jaxpr/psum | solution.py:33
  2291.9 54.5 %all-reduce.14.cloned.1.call-done = f32[8,2816]{1,0:T(8,128)} async-done(((f32[8,2816]{1,0:T(8,128)}), f32[8,2816]{1,0:T(8,128)}) %all-reduce.14.cloned.1.call-update) | async-done | bytes 90128 | tf_op jit(solution)/shard_map/while/body/eval_jaxpr/psum | solution.py:33
  2362.8 54.8 %all-reduce.14.cloned.1.call-done = f32[8,2816]{1,0:T(8,128)} async-done(((f32[8,2816]{1,0:T(8,128)}), f32[8,2816]{1,0:T(8,128)}) %all-reduce.14.cloned.1.call-update) | async-done | bytes 90128 | tf_op jit(solution)/shard_map/while/body/eval_jaxpr/psum | solution.py:33
  2437.8 696.6 %while.88 = (s32[]{:T(128)}, f32[8,704]{1,0:T(8,128)S(1)}, f32[8,704]{1,0:T(8,128)S(1)}, f32[2816]{0:T(1024)S(1)}, bf16[16,8,2816]{1,2,0:T(8,128)(2,1)}, /*index...) while((s32[]{:T(128)}, f32[8,704]{1,0:T(8,128)S(1)}, ...), condition=%wide.region_11.12_spmd.clone, body=%wide.region_8.11_spmd.clone.sunk | while | flops 16163844 | bytes 4291768 | solution.py:60
  2497.6 25.6 all-gather.12
  2541.4 25.6 all-gather.12
  2584.8 25.6 all-gather.12
  2628.6 25.6 all-gather.12
  2671.9 25.6 all-gather.12
  2715.7 25.6 all-gather.12
  2759.0 25.7 all-gather.12
  2802.8 25.6 all-gather.12
  2846.2 25.7 all-gather.12
  2890.0 25.6 all-gather.12
  2933.3 25.7 all-gather.12
  3020.5 25.7 all-gather.12
  3107.7 25.7 all-gather.12
  3144.2 38.2 all-reduce.10.cloned.1.call-done
  3206.8 41.5 %all-gather.16.cloned.1.call-done = f32[16,8,2816]{0,1,2:T(8,128)} async-done(((f32[16,8,352]{0,1,2:T(8,128)}), f32[16,8,2816]{0,1,2:T(8,128)}) %all-gather.16.cloned.1.call-update) | async-done | bytes 1441808 | tf_op jit(solution)/shard_map/all_gather | solution.py:85
  3260.8 667.8 %while.89 = (s32[]{:T(128)}, f32[8,704]{1,0:T(8,128)S(1)}, f32[8,704]{1,0:T(8,128)S(1)}, f32[2816]{0:T(1024)S(1)}, bf16[16,8,2816]{1,2,0:T(8,128)(2,1)}, /*index...) while((s32[]{:T(128)}, f32[8,704]{1,0:T(8,128)S(1)}, ...), condition=%wide.region_16.17_spmd.clone, body=%wide.region_13.16_spmd.clone.sunk | while | flops 16158212 | bytes 4303032 | solution.py:60
  3313.1 25.9 all-gather.13
  3355.6 25.6 all-gather.13
  3397.1 25.9 all-gather.13
  3481.2 25.9 all-gather.13
  3565.3 26.0 all-gather.13
  3607.8 25.6 all-gather.13
  3649.3 26.0 all-gather.13
  3733.4 26.0 all-gather.13
  3817.4 26.0 all-gather.13
  3901.4 26.0 all-gather.13
  (1151 shorter events, 1389.9 us)
Async XLA Ops:
  7.2 1219.3 %copy-start = (bf16[352,2816]{1,0:T(8,128)(2,1)S(1)}, bf16[352,2816]{1,0:T(8,128)(2,1)}, u32[]{:S(2)}) copy-start(bf16[352,2816]{1,0:T(8,128)(2,1)} %param.21) | copy-start | bytes 5947396
  7.2 3.5 copy-start.16
  7.2 4.7 copy-start.15
  7.2 68.3 %all-reduce.6.cloned.1.call-start = ((), (), s32[]{:S(2)}) async-start(), calls=%async_computation | async-start | bytes 2883584 | tf_op jit(solution)/shard_map/psum | solution.py:29
  11.4 0.6 copy-start.11
  12.1 63.4 %copy-start.17 = (f32[2816]{0:T(1024)S(1)}, f32[2816]{0:T(1024)}, u32[]{:S(2)}) copy-start(f32[2816]{0:T(1024)} %param.23) | copy-start | bytes 33796
  81.6 57.2 %all-reduce.12.cloned.1.call-start = ((), (), s32[]{:S(2)}) async-start(), calls=%async_computation.4 | async-start | bytes 180224 | tf_op jit(solution)/shard_map/while/body/eval_jaxpr/psum | solution.py:33
  152.6 58.0 %all-reduce.12.cloned.1.call-start = ((), (), s32[]{:S(2)}) async-start(), calls=%async_computation.4 | async-start | bytes 180224 | tf_op jit(solution)/shard_map/while/body/eval_jaxpr/psum | solution.py:33
  224.4 57.7 %all-reduce.12.cloned.1.call-start = ((), (), s32[]{:S(2)}) async-start(), calls=%async_computation.4 | async-start | bytes 180224 | tf_op jit(solution)/shard_map/while/body/eval_jaxpr/psum | solution.py:33
  295.8 57.7 %all-reduce.12.cloned.1.call-start = ((), (), s32[]{:S(2)}) async-start(), calls=%async_computation.4 | async-start | bytes 180224 | tf_op jit(solution)/shard_map/while/body/eval_jaxpr/psum | solution.py:33
  367.3 57.7 %all-reduce.12.cloned.1.call-start = ((), (), s32[]{:S(2)}) async-start(), calls=%async_computation.4 | async-start | bytes 180224 | tf_op jit(solution)/shard_map/while/body/eval_jaxpr/psum | solution.py:33
  438.8 58.0 %all-reduce.12.cloned.1.call-start = ((), (), s32[]{:S(2)}) async-start(), calls=%async_computation.4 | async-start | bytes 180224 | tf_op jit(solution)/shard_map/while/body/eval_jaxpr/psum | solution.py:33
  510.6 58.0 %all-reduce.12.cloned.1.call-start = ((), (), s32[]{:S(2)}) async-start(), calls=%async_computation.4 | async-start | bytes 180224 | tf_op jit(solution)/shard_map/while/body/eval_jaxpr/psum | solution.py:33
  582.3 58.0 %all-reduce.12.cloned.1.call-start = ((), (), s32[]{:S(2)}) async-start(), calls=%async_computation.4 | async-start | bytes 180224 | tf_op jit(solution)/shard_map/while/body/eval_jaxpr/psum | solution.py:33
  654.1 57.7 %all-reduce.12.cloned.1.call-start = ((), (), s32[]{:S(2)}) async-start(), calls=%async_computation.4 | async-start | bytes 180224 | tf_op jit(solution)/shard_map/while/body/eval_jaxpr/psum | solution.py:33
  725.6 58.0 %all-reduce.12.cloned.1.call-start = ((), (), s32[]{:S(2)}) async-start(), calls=%async_computation.4 | async-start | bytes 180224 | tf_op jit(solution)/shard_map/while/body/eval_jaxpr/psum | solution.py:33
  797.4 57.7 %all-reduce.12.cloned.1.call-start = ((), (), s32[]{:S(2)}) async-start(), calls=%async_computation.4 | async-start | bytes 180224 | tf_op jit(solution)/shard_map/while/body/eval_jaxpr/psum | solution.py:33
  868.8 58.0 %all-reduce.12.cloned.1.call-start = ((), (), s32[]{:S(2)}) async-start(), calls=%async_computation.4 | async-start | bytes 180224 | tf_op jit(solution)/shard_map/while/body/eval_jaxpr/psum | solution.py:33
  940.6 57.7 %all-reduce.12.cloned.1.call-start = ((), (), s32[]{:S(2)}) async-start(), calls=%async_computation.4 | async-start | bytes 180224 | tf_op jit(solution)/shard_map/while/body/eval_jaxpr/psum | solution.py:33
  1012.1 57.7 %all-reduce.12.cloned.1.call-start = ((), (), s32[]{:S(2)}) async-start(), calls=%async_computation.4 | async-start | bytes 180224 | tf_op jit(solution)/shard_map/while/body/eval_jaxpr/psum | solution.py:33
  1083.5 57.7 %all-reduce.12.cloned.1.call-start = ((), (), s32[]{:S(2)}) async-start(), calls=%async_computation.4 | async-start | bytes 180224 | tf_op jit(solution)/shard_map/while/body/eval_jaxpr/psum | solution.py:33
  1155.0 57.7 %all-reduce.12.cloned.1.call-start = ((), (), s32[]{:S(2)}) async-start(), calls=%async_computation.4 | async-start | bytes 180224 | tf_op jit(solution)/shard_map/while/body/eval_jaxpr/psum | solution.py:33
  1226.5 62.2 %all-reduce.8.cloned.1.call-start = ((), (), s32[]{:S(2)}) async-start(), calls=%async_computation.1 | async-start | bytes 2883584 | tf_op jit(solution)/shard_map/psum | solution.py:29
  1226.5 2.7 copy-start.13
  1226.5 2.7 copy-start.3
  1226.5 62.1 %copy-start.18 = (f32[2816]{0:T(1024)S(1)}, f32[2816]{0:T(1024)}, u32[]{:S(2)}) copy-start(f32[2816]{0:T(1024)} %param.24) | copy-start | bytes 33796
  1294.7 56.7 %all-reduce.14.cloned.1.call-start = ((), (), s32[]{:S(2)}) async-start(), calls=%async_computation.5 | async-start | bytes 180224 | tf_op jit(solution)/shard_map/while/body/eval_jaxpr/psum | solution.py:33
  1365.2 57.1 %all-reduce.14.cloned.1.call-start = ((), (), s32[]{:S(2)}) async-start(), calls=%async_computation.5 | async-start | bytes 180224 | tf_op jit(solution)/shard_map/while/body/eval_jaxpr/psum | solution.py:33
  1436.1 57.4 %all-reduce.14.cloned.1.call-start = ((), (), s32[]{:S(2)}) async-start(), calls=%async_computation.5 | async-start | bytes 180224 | tf_op jit(solution)/shard_map/while/body/eval_jaxpr/psum | solution.py:33
  1507.3 57.4 %all-reduce.14.cloned.1.call-start = ((), (), s32[]{:S(2)}) async-start(), calls=%async_computation.5 | async-start | bytes 180224 | tf_op jit(solution)/shard_map/while/body/eval_jaxpr/psum | solution.py:33
  1578.5 57.4 %all-reduce.14.cloned.1.call-start = ((), (), s32[]{:S(2)}) async-start(), calls=%async_computation.5 | async-start | bytes 180224 | tf_op jit(solution)/shard_map/while/body/eval_jaxpr/psum | solution.py:33
  1649.7 57.1 %all-reduce.14.cloned.1.call-start = ((), (), s32[]{:S(2)}) async-start(), calls=%async_computation.5 | async-start | bytes 180224 | tf_op jit(solution)/shard_map/while/body/eval_jaxpr/psum | solution.py:33
  1720.6 57.4 %all-reduce.14.cloned.1.call-start = ((), (), s32[]{:S(2)}) async-start(), calls=%async_computation.5 | async-start | bytes 180224 | tf_op jit(solution)/shard_map/while/body/eval_jaxpr/psum | solution.py:33
  1791.7 57.1 %all-reduce.14.cloned.1.call-start = ((), (), s32[]{:S(2)}) async-start(), calls=%async_computation.5 | async-start | bytes 180224 | tf_op jit(solution)/shard_map/while/body/eval_jaxpr/psum | solution.py:33
  1862.6 57.1 %all-reduce.14.cloned.1.call-start = ((), (), s32[]{:S(2)}) async-start(), calls=%async_computation.5 | async-start | bytes 180224 | tf_op jit(solution)/shard_map/while/body/eval_jaxpr/psum | solution.py:33
  1933.6 57.4 %all-reduce.14.cloned.1.call-start = ((), (), s32[]{:S(2)}) async-start(), calls=%async_computation.5 | async-start | bytes 180224 | tf_op jit(solution)/shard_map/while/body/eval_jaxpr/psum | solution.py:33
  2004.8 57.4 %all-reduce.14.cloned.1.call-start = ((), (), s32[]{:S(2)}) async-start(), calls=%async_computation.5 | async-start | bytes 180224 | tf_op jit(solution)/shard_map/while/body/eval_jaxpr/psum | solution.py:33
  2076.0 57.1 %all-reduce.14.cloned.1.call-start = ((), (), s32[]{:S(2)}) async-start(), calls=%async_computation.5 | async-start | bytes 180224 | tf_op jit(solution)/shard_map/while/body/eval_jaxpr/psum | solution.py:33
  2146.8 57.4 %all-reduce.14.cloned.1.call-start = ((), (), s32[]{:S(2)}) async-start(), calls=%async_computation.5 | async-start | bytes 180224 | tf_op jit(solution)/shard_map/while/body/eval_jaxpr/psum | solution.py:33
  2218.0 57.4 %all-reduce.14.cloned.1.call-start = ((), (), s32[]{:S(2)}) async-start(), calls=%async_computation.5 | async-start | bytes 180224 | tf_op jit(solution)/shard_map/while/body/eval_jaxpr/psum | solution.py:33
  2289.2 57.1 %all-reduce.14.cloned.1.call-start = ((), (), s32[]{:S(2)}) async-start(), calls=%async_computation.5 | async-start | bytes 180224 | tf_op jit(solution)/shard_map/while/body/eval_jaxpr/psum | solution.py:33
  2360.1 57.4 %all-reduce.14.cloned.1.call-start = ((), (), s32[]{:S(2)}) async-start(), calls=%async_computation.5 | async-start | bytes 180224 | tf_op jit(solution)/shard_map/while/body/eval_jaxpr/psum | solution.py:33
  2431.3 751.0 %all-reduce.10.cloned.1.call-start = ((), (), s32[]{:S(2)}) async-start(), calls=%async_computation.2 | async-start | bytes 393216 | tf_op jit(solution)/shard_map/psum | solution.py:85
  2431.3 6.5 copy-start.5
  2431.3 6.5 copy-start.7
  3134.5 9.6 copy-start.8
  3144.0 40.9 %copy-start.4 = (bf16[16,8,352]{2,1,0:T(8,128)(2,1)S(1)}, bf16[16,8,352]{2,1,0:T(8,128)(2,1)}, u32[]{:S(2)}) copy-start(bf16[16,8,352]{2,1,0:T(8,128)(2,1)} %get-tuple-element.696) | copy-start | bytes 270340
  3144.1 104.2 %all-gather.16.cloned.1.call-start = ((), (), s32[]{:S(2)}) async-start(), calls=%async_computation.3 | async-start | bytes 12976128 | tf_op jit(solution)/shard_map/all_gather | solution.py:85
  3185.0 9.5 copy-start.6
  3185.0 9.5 copy-start.14
  3254.2 6.6 copy-start.2
  3928.5 9.3 copy-start.9
  3928.5 9.3 copy-start.10
  3937.9 9.2 copy-start.12
  3947.0 2.7 copy-start.1
Sparse Core Ops, SparseCore 0:
  11.0 64.4 all-reduce.5
  85.3 53.4 all-reduce.11
  156.3 54.1 all-reduce.11
  227.8 54.1 all-reduce.11
  299.3 54.1 all-reduce.11
  370.7 54.1 all-reduce.11
  442.5 54.1 all-reduce.11
  514.3 54.1 all-reduce.11
  586.1 54.1 all-reduce.11
  657.5 54.1 all-reduce.11
  729.3 54.1 all-reduce.11
  800.8 54.1 all-reduce.11
  872.6 54.1 all-reduce.11
  944.1 54.1 all-reduce.11
  1015.5 54.1 all-reduce.11
  1087.0 54.1 all-reduce.11
  1158.4 54.1 all-reduce.11
  1229.9 58.6 all-reduce.7
  1297.9 53.4 all-reduce.13
  1368.0 54.1 all-reduce.13
  1439.2 54.1 all-reduce.13
  1510.4 54.1 all-reduce.13
  1581.6 54.1 all-reduce.13
  1652.5 54.1 all-reduce.13
  1723.7 54.1 all-reduce.13
  1794.6 54.1 all-reduce.13
  1865.5 54.1 all-reduce.13
  1936.7 54.1 all-reduce.13
  2007.9 54.1 all-reduce.13
  2078.8 54.1 all-reduce.13
  2150.0 54.1 all-reduce.13
  2221.2 54.1 all-reduce.13
  2292.1 54.1 all-reduce.13
  2363.3 54.1 all-reduce.13
  3144.2 38.1 all-reduce.9
  3185.0 63.1 all-gather.15
where the time goes:
time: 3970 us; the launch traced here: 3960 us
  waiting for transfers between devices  1930 us (49%)
  blocking collectives  1520 us (38%)
  local copies, waits for them, and re-layouts  197 us (5%)
  matrix products  167 us (4%)
  other arithmetic  128 us (3%)
    psum x32, waiting for transfers between devices, step_fn(): lax.psum(jnp.dot(h_rows, w_rec, preferred_element_type=jnp.float32), 'row')  1760 us
    all_gather x32, blocking collectives, step_fn(): lax.all_gather(lax.psum(row_part, 'col'), 'row', axis=1, tiled=True)  813 us
    psum x32, blocking collectives, step_fn(): lax.psum(row_part, 'col')  364 us
    all_gather x32, blocking collectives, step_fn(): h_full = lax.all_gather(h_cols, 'col', axis=1, tiled=True)  310 us
    psum x2, waiting for transfers between devices, layer_forward(): lax.psum(jnp.einsum('tbk,kn->tbn', in_rows, w_in, preferred_element_type=...  90 us
    dot_general x32, matrix products, step_fn(): jnp.dot(h_rows, w_rec, preferred_element_type=jnp.float32)  81.9 us
  transfers between devices with their start and end apart: 36, of which 36 were waited for; matrix products, arithmetic and copies ran while one was open for 1% of the time, Pallas kernels for 0%

commit v1 on v0

v1 whole, which is shorter than its diff:
```python
import functools

import jax
import jax.numpy as jnp
from jax import lax
from jax.experimental import pallas as pl
from jax.experimental.pallas import tpu as pltpu
from jax.sharding import PartitionSpec as P

MESH = pl.DeviceIdType.MESH
F32 = jnp.float32
BF16 = jnp.bfloat16
LANE = 128
WIN = 512


def dot(a, b):
    return jnp.dot(a, b, preferred_element_type=F32)


def dot_t(a, b):
    return lax.dot_general(a, b, (((1,), (1,)), ((), ())), preferred_element_type=F32)


def lane_iota(rows):
    return lax.broadcasted_iota(jnp.int32, (rows, LANE), 1)


def join(get, first, count, unit, rows):
    lane = lane_iota(rows)
    tiles = []
    for q in range(-(-count * unit // LANE)):
        lo = q * LANE
        val = get(first + lo // unit)
        for d in range(lo // unit + 1, min((lo + LANE - 1) // unit + 1, count)):
            val = jnp.where(lane >= unit * d - lo, get(first + d), val)
        tiles.append(val)
    return jnp.concatenate(tiles, axis=1)


def split_gates(z, unit):
    lane = lane_iota(z.shape[0])
    tiles = [z[:, q * LANE:(q + 1) * LANE] for q in range(z.shape[1] // LANE)]
    out = []
    for k in range(4):
        q, s = divmod(k * unit, LANE)
        a = tiles[q]
        if s == 0:
            out.append(a)
            continue
        a = pltpu.roll(a, LANE - s, 1)
        if s + unit > LANE:
            a = jnp.where(lane < LANE - s, a, pltpu.roll(tiles[q + 1], LANE - s, 1))
        out.append(a)
    return out


def pack_gates(parts, unit, n_tiles):
    rows = parts[0].shape[0]
    lane = lane_iota(rows)
    rolled = [p if (k * unit) % LANE == 0 else pltpu.roll(p, (k * unit) % LANE, 1) for k, p in enumerate(parts)]
    tiles = []
    for q in range(n_tiles):
        lo = q * LANE
        val = jnp.zeros_like(parts[0])
        for k in range(4):
            a, b = k * unit - lo, (k + 1) * unit - lo
            if b <= 0 or a >= LANE:
                continue
            keep = (lane >= a) & (lane < b)
            val = jnp.where(keep, rolled[k], val)
        tiles.append(val)
    return jnp.concatenate(tiles, axis=1)


def recur_kernel(C, R, T, B, U,
                 x_ref, wx1, wh1, wx2, wh2, bias_ref, h0_ref, c0_ref, g_ref,
                 left_ref, dzn_ref, gb_ref,
                 pm, stage, wf, wt, xs, xr, u1, hist1, hist2, sv, c_in, cst, part, r1, r2, s1, s2,
                 dza, dzacc, gbacc, gbbuf, pxs, zscr, dcs,
                 ws, wr, xss, xrs, css, crs, h1s, h1r, h2s, h2r, b1s, b1r, b2s, b2r, dzs, dzr, gbs, gbr):
    N = C * R
    unit = U // N
    rows = U // R
    cols = 4 * U // C
    ncol = 4 * unit
    npad = stage.shape[-1]
    c = lax.axis_index('col')
    r = lax.axis_index('row')
    me = c * R + r
    my_s = lax.rem(me * unit, LANE)

    def dev(p):
        return {'col': p // R, 'row': lax.rem(p, R)}

    bar = pltpu.get_barrier_semaphore()
    for k in range(1, N):
        pl.semaphore_signal(bar, inc=1, device_id=dev(lax.rem(me + k, N)), device_id_type=MESH)

    def start(src, dst, ss, rs, did):
        pltpu.make_async_remote_copy(src_ref=src, dst_ref=dst, send_sem=ss, recv_sem=rs, device_id=did, device_id_type=MESH).start()

    def wait(ref, sem):
        pltpu.make_async_copy(ref, ref, sem).wait()

    def win(p):
        return pl.multiple_of(jnp.minimum((p * ncol) // LANE * LANE, cols - WIN), LANE)

    kk = lax.broadcasted_iota(jnp.int32, (WIN, npad), 0)
    nn = lax.broadcasted_iota(jnp.int32, (WIN, npad), 1)
    gate = (nn >= unit).astype(jnp.int32) + (nn >= 2 * unit).astype(jnp.int32) + (nn >= 3 * unit).astype(jnp.int32)
    target = jnp.where(nn < ncol, 4 * (nn - unit * gate) + gate, -cols) - kk

    def regroup(w, slot, k):
        p = lax.rem(r + k, R)
        return dot(w[:, pl.ds(win(p), WIN)], pm[p]).astype(BF16)

    my_rows = pl.ds(pl.multiple_of(r * rows, 16), rows)

    def make_pm(k, _):
        p = lax.rem(r + k, R)
        pm[p] = jnp.where(target == win(p) - p * ncol, 1.0, 0.0).astype(BF16)
        stage[0, p] = regroup(wh1, 0, k)
        return 0

    lax.fori_loop(0, R, make_pm, 0)
    pl.semaphore_wait(bar, N - 1)

    def send_w(w):
        def body(k, _):
            p = lax.rem(r + k, R)
            start(stage.at[w, p], wf.at[w, my_rows], ws.at[w], wr.at[w], {'col': c, 'row': p})
            return 0
        lax.fori_loop(1, R, body, 0)
        wf[w, my_rows] = stage[w, r]

    send_w(0)

    owner = r * (N // R) + c

    @pl.when(owner != me)
    def _():
        start(c0_ref, c_in, css, crs, dev(owner))

    @pl.when(owner == me)
    def _():
        c_in[...] = c0_ref[...]

    def xproj(k, _):
        p = lax.rem(r + k, R)
        stage[1, p] = regroup(wh2, 1, k)
        xs[p, pl.ds(0, T * B)] = dot(x_ref[...], regroup(wx1, 0, k))
        xs[p, pl.ds(0, B)] += dot(h0_ref[0], stage[0, p])
        xs[p, pl.ds(T * B, B)] = dot(h0_ref[1], stage[1, p])

        @pl.when(k > 0)
        def _():
            start(xs.at[p], xr.at[r], xss, xrs, {'col': c, 'row': p})
        return 0

    lax.fori_loop(0, R, xproj, 0)
    xr[r] = xs[r]
    send_w(1)

    def third(k, _):
        p = lax.rem(r + k, R)
        stage[2, p] = regroup(wx2, 2, k)
        return 0

    lax.fori_loop(0, R, third, 0)
    send_w(2)

    def wait_w(w):
        wait(stage.at[w, pl.ds(0, R - 1)], wr.at[w])

    wait(xr.at[pl.ds(0, R - 1)], xrs)
    acc = xr[0]
    for k in range(1, R):
        acc = acc + xr[k]
    u1[...] = acc.reshape(T + 1, B, npad)

    @pl.when(owner != me)
    def _():
        wait(c_in, crs)
    cst[...] = c_in[...]

    def transpose_w(w):
        eye = (lax.broadcasted_iota(jnp.int32, (npad, npad), 0) == lax.broadcasted_iota(jnp.int32, (npad, npad), 1))
        eye = jnp.where(eye, 1.0, 0.0).astype(BF16)

        def body(k, _):
            off = pl.multiple_of(k * 256, 256)
            wt[w, :, pl.ds(off, 256)] = dot_t(eye, wf[w, pl.ds(off, 256)]).astype(BF16)
            return 0
        lax.fori_loop(0, U // 256, body, 0)

    def cell(layer, t, z):
        zi, zf, zg, zo = split_gates(z, unit)
        gi, gf, gg, go = jax.nn.sigmoid(zi), jax.nn.sigmoid(zf), jnp.tanh(zg), jax.nn.sigmoid(zo)
        c_prev = cst[layer]
        c_new = gf * c_prev + gi * gg
        tc = jnp.tanh(c_new)
        cst[layer] = c_new
        for k, v in enumerate((gi, gf, gg, go, c_prev, tc)):
            sv[layer, t, k] = v
        return pltpu.roll(go * tc, my_s, 1).astype(BF16)

    def bcast(hist, t, ss, rs):
        for k in range(1, N):
            start(hist.at[t, me], hist.at[t, me], ss.at[t], rs.at[t], dev(lax.rem(me + k, N)))

    def gathered(hist, t):
        return join(lambda d: hist[t, d].astype(F32), 0, N, unit, B).astype(BF16)

    hist1[0, me] = cell(0, 0, u1[0] + bias_ref[0])
    bcast(hist1, 0, h1s, h1r)
    wait_w(0)
    wait_w(1)
    wait_w(2)

    def fwd(s, _):
        wait(hist1.at[s, pl.ds(0, N - 1)], h1r.at[s])
        h_full = gathered(hist1, s)

        @pl.when(s < T - 1)
        def _():
            hist1[s + 1, me] = cell(0, s + 1, u1[s + 1] + bias_ref[0] + dot(h_full, wf[0]))
            bcast(hist1, s + 1, h1s, h1r)

        zx = dot(h_full, wf[2]) + bias_ref[1]

        @pl.when(s == 0)
        def _():
            zscr[...] = u1[T]

        @pl.when(s > 0)
        def _():
            wait(hist2.at[s - 1, pl.ds(0, N - 1)], h2r.at[s - 1])
            zscr[...] = dot(gathered(hist2, s - 1), wf[1])

        hist2[s, me] = cell(1, s, zx + zscr[...])

        @pl.when(s < T - 1)
        def _():
            bcast(hist2, s, h2s, h2r)

        for w in range(3):
            @pl.when(s == w + 2)
            def _():
                transpose_w(w)
        return 0

    lax.fori_loop(0, T, fwd, 0)

    gbacc[...] = jnp.zeros_like(gbacc)
    dcs[...] = jnp.zeros_like(dcs)

    def cell_grad(layer, t, dh):
        gi, gf, gg, go, c_prev, tc = [sv[layer, t, k] for k in range(6)]
        dc = dcs[layer] + dh * go * (1.0 - tc * tc)
        dz = (dc * gg * gi * (1.0 - gi), dc * c_prev * gf * (1.0 - gf), dc * gi * (1.0 - gg * gg), dh * tc * go * (1.0 - go))
        dcs[layer] = dc * gf
        for k in range(4):
            gbacc[layer, k] += dz[k]
        packed = pack_gates(dz, unit, npad // LANE).astype(BF16)
        dza[layer, r, t] = packed
        return packed

    lane_b = lane_iota(B)

    def scatter(p, sbuf, rbuf, t, ss, rs):
        tiles = [p[:, q * LANE:(q + 1) * LANE] for q in range(U // LANE)]
        for d in range(N):
            q, s = divmod(d * unit, LANE)
            v = tiles[q]
            if s + unit > LANE:
                v = jnp.where(lane_b >= s, v, tiles[q + 1])
            sbuf[t, d] = v
        for k in range(1, N):
            d = lax.rem(me + k, N)
            start(sbuf.at[t, d], rbuf.at[t, me], ss.at[t], rs.at[t], dev(d))
        rbuf[t, me] = sbuf[t, me]

    def reduced(rbuf, t, rs):
        wait(rbuf.at[t, pl.ds(0, N - 1)], rs.at[t])
        vals = [rbuf[t, d] for d in range(N)]
        while len(vals) > 1:
            vals = [a + b for a, b in zip(vals[::2], vals[1::2])]
        return pltpu.roll(vals[0], lax.rem(LANE - my_s, LANE), 1)

    CH = 4

    def send_dz(layer, t):
        @pl.when(lax.rem(t, CH) == 0)
        def _():
            ts = pl.ds(t, CH)
            for k in range(1, R):
                start(dza.at[layer, r, ts], dza.at[layer, r, ts], dzs.at[layer, t // CH], dzr.at[layer, t // CH],
                      {'col': c, 'row': lax.rem(r + k, R)})

    def bwd(s, _):
        t = T - 1 - s
        part[...] = g_ref[t].astype(F32)

        @pl.when(s > 0)
        def _():
            part[...] += reduced(r2, t, b2r)

        dz2 = cell_grad(1, t, part[...])

        @pl.when(t > 0)
        def _():
            scatter(dot(dz2, wt[1]), s2, r2, t - 1, b2s, b2r)

        pxs[...] = dot(dz2, wt[2])
        send_dz(1, t)

        @pl.when(s > 0)
        def _():
            dz1 = cell_grad(0, t + 1, reduced(r1, t + 1, b1r))
            pxs[...] += dot(dz1, wt[0])

        scatter(pxs[...], s1, r1, t, b1s, b1r)

        @pl.when(s > 0)
        def _():
            send_dz(0, t + 1)
        return 0

    lax.fori_loop(0, T, bwd, 0)
    cell_grad(0, 0, reduced(r1, 0, b1r))
    send_dz(0, 0)

    sub = lax.broadcasted_iota(jnp.int32, (8, LANE), 0)
    packed = []
    for k in range(4):
        b0 = jnp.sum(gbacc[0, k], axis=0, keepdims=True)
        b1 = jnp.sum(gbacc[1, k], axis=0, keepdims=True)
        packed.append(jnp.where(sub == 0, jnp.broadcast_to(b0, (8, LANE)), jnp.broadcast_to(b1, (8, LANE))))
    gbbuf[r] = pack_gates(packed, unit, npad // LANE)
    for k in range(1, R):
        start(gbbuf.at[r], gbbuf.at[r], gbs, gbr, {'col': c, 'row': lax.rem(r + k, R)})

    shift = lax.rem(LANE * rows - r * rows, LANE)
    per = N // R

    def local_rows(hist, count):
        def get(d):
            v = hist[pl.ds(0, count), per * r + d].astype(F32).reshape(count * B, LANE)
            return pltpu.roll(v, shift, 1)
        return join(get, 0, per, unit, count * B)

    h1_rows = local_rows(hist1, T)
    h2_rows = local_rows(hist2, T - 1)

    def h0_rows(layer):
        return jnp.concatenate([h0_ref[layer].astype(F32), jnp.zeros((B, npad - rows), F32)], axis=1)

    left_ref[0] = jnp.concatenate([h0_rows(0), h1_rows[:(T - 1) * B]], axis=0).astype(BF16)
    left_ref[1] = h1_rows.astype(BF16)
    left_ref[2] = jnp.concatenate([h0_rows(1), h2_rows], axis=0).astype(BF16)

    for layer in (1, 0):
        for q in range(T // CH):
            wait(dza.at[layer, pl.ds(0, R - 1), pl.ds(0, CH)], dzr.at[layer, q])
        dzacc[...] = jnp.zeros_like(dzacc)
        for p in range(R):
            st = min(p * ncol // LANE * LANE, cols - WIN)
            dzp = dza[layer, p].astype(F32).reshape(T * B, npad).astype(BF16)
            dzacc[:, st:st + WIN] += dot_t(dzp, pm[p])
        dzn_ref[layer] = dzacc[...].astype(BF16)
    wait(gbbuf.at[pl.ds(0, R - 1)], gbr)
    gb_ref[...] = gbbuf[...]

    for w in range(3):
        wait(stage.at[w, pl.ds(0, R - 1)], ws.at[w])
    wait(xs.at[pl.ds(0, R - 1)], xss)

    @pl.when(owner != me)
    def _():
        wait(c_in, css)

    def drain(t, _):
        wait(hist1.at[t, pl.ds(0, N - 1)], h1s.at[t])
        wait(s1.at[t, pl.ds(0, N - 1)], b1s.at[t])

        @pl.when(t < T - 1)
        def _():
            wait(hist2.at[t, pl.ds(0, N - 1)], h2s.at[t])
            wait(s2.at[t, pl.ds(0, N - 1)], b2s.at[t])
        return 0

    lax.fori_loop(0, T, drain, 0)
    for layer in range(2):
        for q in range(T // CH):
            wait(dza.at[layer, pl.ds(0, R - 1), pl.ds(0, CH)], dzs.at[layer, q])
    wait(gbbuf.at[pl.ds(0, R - 1)], gbs)


def grad_kernel(x_ref, left_ref, dzn_ref, gx1, gh1, gx2, gh2):
    rows = gx1.shape[0]
    tn = (((0,), (0,)), ((), ()))

    def mm(a, b):
        return lax.dot_general(a, b, tn, preferred_element_type=F32)

    gx1[...] = mm(x_ref[...], dzn_ref[0])
    gh1[...] = mm(left_ref[0], dzn_ref[0])[:rows]
    gx2[...] = mm(left_ref[1], dzn_ref[1])[:rows]
    gh2[...] = mm(left_ref[2], dzn_ref[1])[:rows]


def solution(mesh):
    C, R = mesh.shape['col'], mesh.shape['row']
    N = C * R
    seq_spec = P(None, 'data', 'row')
    w_spec = P('row', 'col')
    bias_spec = P('col')
    g_spec = P(None, 'data', 'col')
    grad_spec = P(('data', 'row'), 'col')
    gbias_spec = P(('data', 'col'))

    def local_grads(seq_in, w_x1, w_h1, w_x2, w_h2, bias_1, bias_2, h_init, c_init, g_out):
        T, B, rows = seq_in.shape
        U = rows * R
        cols = w_x1.shape[1]
        unit = U // N
        ncol = 4 * unit
        nt = -(-ncol // LANE)
        npad = nt * LANE
        r = lax.axis_index('row')
        c = lax.axis_index('col')

        x2d = seq_in.reshape(T * B, rows)
        h0 = h_init.astype(BF16)
        c0 = jnp.pad(lax.dynamic_slice_in_dim(c_init, c * unit, unit, axis=2), ((0, 0), (0, 0), (0, LANE - unit)))
        g = jnp.pad(lax.dynamic_slice_in_dim(g_out, r * unit, unit, axis=2), ((0, 0), (0, 0), (0, LANE - unit)))
        bias = lax.dynamic_slice_in_dim(jnp.stack([bias_1, bias_2]), r * ncol, ncol, axis=1)
        bias = jnp.swapaxes(bias.reshape(2, unit, 4), 1, 2).reshape(2, 1, ncol)
        bias = jnp.broadcast_to(jnp.pad(bias, ((0, 0), (0, 0), (0, npad - ncol))), (2, B, npad))

        vm = pl.BlockSpec(memory_space=pltpu.VMEM)
        dma = pltpu.SemaphoreType.DMA
        V = pltpu.VMEM
        left, dzn, gb = pl.pallas_call(
            functools.partial(recur_kernel, C, R, T, B, U),
            name='recur',
            out_shape=(jax.ShapeDtypeStruct((3, T * B, npad), BF16), jax.ShapeDtypeStruct((2, T * B, cols), BF16),
                       jax.ShapeDtypeStruct((R, 8, npad), F32)),
            in_specs=[vm] * 9,
            out_specs=(vm, vm, vm),
            scratch_shapes=[
                V((R, WIN, npad), BF16),
                V((3, R, rows, npad), BF16),
                V((3, U, npad), BF16),
                V((3, npad, U), BF16),
                V((R, (T + 1) * B, npad), F32),
                V((R, (T + 1) * B, npad), F32),
                V((T + 1, B, npad), F32),
                V((T, N, B, LANE), BF16),
                V((T, N, B, LANE), BF16),
                V((2, T, 6, B, LANE), F32),
                V((2, B, LANE), F32),
                V((2, B, LANE), F32),
                V((B, LANE), F32),
                V((T, N, B, LANE), F32),
                V((T, N, B, LANE), F32),
                V((T, N, B, LANE), F32),
                V((T, N, B, LANE), F32),
                V((2, R, T, B, npad), BF16),
                V((T * B, cols), F32),
                V((2, 4, B, LANE), F32),
                V((R, 8, npad), F32),
                V((B, U), F32),
                V((B, npad), F32),
                V((2, B, LANE), F32),
                dma((3,)), dma((3,)), dma, dma, dma, dma,
                dma((T,)), dma((T,)), dma((T,)), dma((T,)),
                dma((T,)), dma((T,)), dma((T,)), dma((T,)),
                dma((2, T // 4)), dma((2, T // 4)), dma, dma,
            ],
            compiler_params=pltpu.CompilerParams(collective_id=0, has_side_effects=True, vmem_limit_bytes=62 * 1024 * 1024),
        )(x2d, w_x1, w_h1, w_x2, w_h2, bias, h0, c0, g)

        tn = 256
        out = jax.ShapeDtypeStruct((rows, cols), F32)
        ospec = pl.BlockSpec((rows, tn), lambda i: (0, i))
        grads = pl.pallas_call(
            grad_kernel,
            name='grads',
            grid=(cols // tn,),
            out_shape=(out,) * 4,
            in_specs=[pl.BlockSpec((T * B, rows), lambda i: (0, 0)), pl.BlockSpec((3, T * B, npad), lambda i: (0, 0, 0)),
                      pl.BlockSpec((2, T * B, tn), lambda i: (0, 0, i))],
            out_specs=(ospec,) * 4,
        )(x2d, left, dzn)
        gbt = jnp.swapaxes(gb[:, :2, :ncol].reshape(R, 2, 4, unit), 2, 3)
        gb1 = gbt[:, 0].reshape(cols)
        gb2 = gbt[:, 1].reshape(cols)
        return (*grads, gb1, gb2)

    return jax.shard_map(local_grads, mesh=mesh,
                         in_specs=(seq_spec, w_spec, w_spec, w_spec, w_spec, bias_spec, bias_spec, seq_spec, seq_spec, g_spec),
                         out_specs=(grad_spec, grad_spec, grad_spec, grad_spec, gbias_spec, gbias_spec),
                         check_vma=False)
```

time: 3970 us -> 312 us (0.08)
  waiting for transfers between devices: 1930 us -> 0 us
  blocking collectives: 1520 us -> 0 us
  Pallas kernels: 0 us -> 302 us
  local copies, waits for them, and re-layouts: 197 us -> 7.43 us
  matrix products: 167 us -> 0 us
  other arithmetic: 128 us -> 1.42 us
    psum x35 -> x0, waiting for transfers between devices: 1880 us -> none  [the longest x32 1760 us: step_fn(): lax.psum(jnp.dot(h_rows, w_rec, preferred_element_type=jnp.float32), 'row')]
    all_gather x65 -> x0, blocking collectives: 1150 us -> none  [the longest x32 813 us: step_fn(): lax.all_gather(lax.psum(row_part, 'col'), 'row', axis=1, tiled=True)]
    psum x32 -> x0, blocking collectives: 364 us -> none  [step_fn(): lax.psum(row_part, 'col')]
    pallas_call x0 -> x2, Pallas kernels: none -> 302 us  [the longest x1 292 us: local_grads(): pl.pallas_call(functools.partial(recur_kernel, C, R, T, B, U), name='recu...]
    dot_general x71 -> x0, matrix products: 167 us -> none  [the longest x32 81.9 us: step_fn(): jnp.dot(h_rows, w_rec, preferred_element_type=jnp.float32)]
    dynamic_update_slice x64 -> x0, local copies, waits for them, and re-layouts: 50.9 us -> none  [the longest x32 29.5 us: layer_backward(): lax.scan(step_fn, zero_carry, (dh_seq, gate_seq, c_prev_seq, tanh_seq), r...]
    all_gather x1 -> x0, waiting for transfers between devices: 41.5 us -> none  [local_grads(): lax.all_gather(lax.psum(dh_part, 'col'), 'row', axis=2, tiled=True)]
    dynamic_update_slice x64 -> x0, other arithmetic: 40.9 us -> none  [layer_forward(): return lax.scan(step_fn, (h_start, c_start), projected)[1]]
  transfers between devices with their start and end apart: 36 -> 0, of which waited for: 36 -> 0; matrix products, arithmetic and copies ran while one was open for 1% -> 0% of each run, Pallas kernels for 0% -> 0%
where the time goes in v1:
time: 312 us
  Pallas kernels  302 us (97%)
  local copies, waits for them, and re-layouts  7.43 us (2%)
    pallas_call x1, Pallas kernels, local_grads(): pl.pallas_call(functools.partial(recur_kernel, C, R, T, B, U), name='recu...  292 us
    pallas_call x1, Pallas kernels, local_grads(): pl.pallas_call(grad_kernel, name='grads', grid=(cols // tn,), out_shape=(...  10.2 us

profile of v1, /device:TPU:97, one launch (start us, length us, event | category | flops | bytes accessed | tf_op | source)
XLA Modules:
  0.0 311.9 jit_solution(15740195181775455297)
XLA Ops:
  0.6 0.0 copy-start
  0.7 0.8 constant_dynamic-slice_fusion.1
  1.5 0.6 pad.13.c0_ref
  2.1 0.7 stack.9
  2.8 0.7 stack.10
  3.5 0.1 fusion
  3.6 1.3 convert_element_type.9.h0_ref
  4.9 0.0 copy-done
  4.9 0.1 constant_dynamic-slice_fusion
  5.0 0.6 pad.14.g_ref
  5.7 0.1 reshape.25
  5.8 0.1 copy.17
  5.8 0.1 reshape.26
  6.0 0.6 broadcast_in_dim.8.bias_ref
  6.6 292.2 %recur.1 = (bf16[3,128,384]{2,1,0:T(8,128)(2,1)}, bf16[2,128,2816]{2,1,0:T(8,128)(2,1)}, f32[8,8,384]{2,1,0:T(8,128)}) custom-call(bf16[128,352]{1,0:T(8,128)(2,1)} %bitcast.14, bf16[352,2816]{1,0:T(8,128)(2,1)} %wx1.1, bf16[352,2816]{1,0:T(8,128)(2,1)} %wh1.1, bf16[352,2816]{1,0:T(8,128)(2,1)} %wx2.1, bf16[352,2816]{1,0:T(8,128)(2,1)} %wh2.1, ...), custom_call_target="tpu_custom_call" | custom-call | tf_op jit(solution)/shard_map/recur/pallas_call | solution.py:445
  298.7 0.9 slice.9
  299.6 0.1 reshape.27
  299.7 0.3 copy.18
  300.1 0.8 reshape_squeeze.7
  300.9 0.8 reshape_squeeze.6
  301.7 10.2 %grads.1 = (f32[352,2816]{1,0:T(8,128)}, f32[352,2816]{1,0:T(8,128)}, f32[352,2816]{1,0:T(8,128)}, f32[352,2816]{1,0:T(8,128)}) custom-call(bf16[128,352]{1,0:T(8,128)(2,1)} %bitcast.15, bf16[3,128,384]{2,1,0:T(8,128)(2,1)} %get-tuple-element.13.left_ref, bf16[2,128,2816]{2,1,0:T(8,128)(2,1)} %get-tuple-element.14.dzn_ref), custom_call_target="tpu_custom_call" | custom-call | tf_op jit(solution)/shard_map/grads/pallas_call | solution.py:488
  (2 shorter events, 0.1 us)
Async XLA Ops:
  0.6 4.3 %copy-start = (bf16[16,8,704]{2,1,0:T(8,128)(2,1)S(1)}, bf16[16,8,704]{2,1,0:T(8,128)(2,1)}, u32[]{:S(2)}) copy-start(bf16[16,8,704]{2,1,0:T(8,128)(2,1)} %param.19) | copy-start | bytes 540676

commit v2 on v1

v2 whole, which is shorter than its diff:
```python
import functools

import jax
import jax.numpy as jnp
from jax import lax
from jax.experimental import pallas as pl
from jax.experimental.pallas import tpu as pltpu
from jax.sharding import PartitionSpec as P

MESH = pl.DeviceIdType.MESH
F32 = jnp.float32
BF16 = jnp.bfloat16
LANE = 128
WIN = 512
CH = 4
X_CUTS = (0, 6, 9, 12, 16)
X_SEND = (None, 2, 4, 6)
W2_CUTS = (0, 128, 240, 352)
GROWS = 4
WROWS = 32


def dot(a, b):
    return jnp.dot(a, b, preferred_element_type=F32)


def dot_t(a, b):
    return lax.dot_general(a, b, (((1,), (1,)), ((), ())), preferred_element_type=F32)


def by_thirds(x, f):
    x = x * 0.25
    hi = x.astype(BF16)
    rest = x - hi.astype(F32)
    mid = rest.astype(BF16)
    lo = (rest - mid.astype(F32)).astype(BF16)
    return ((f(hi) + f(mid)) + f(lo)) * 4.0


def lane_iota(rows):
    return lax.broadcasted_iota(jnp.int32, (rows, LANE), 1)


def join(segs, width):
    lane = lane_iota(segs[0][1].shape[0])
    tiles = []
    for lo in range(0, width, LANE):
        val = None
        for i, (start, tile) in enumerate(segs):
            end = segs[i + 1][0] if i + 1 < len(segs) else width
            if end <= lo or start >= lo + LANE:
                continue
            val = tile if val is None else jnp.where(lane >= start - lo, tile, val)
        tiles.append(val)
    return jnp.concatenate(tiles, axis=1)


def split_gates(z, unit):
    lane = lane_iota(z.shape[0])
    tiles = [z[:, q * LANE:(q + 1) * LANE] for q in range(z.shape[1] // LANE)]
    out = []
    for k in range(4):
        q, s = divmod(k * unit, LANE)
        a = tiles[q]
        if s:
            a = pltpu.roll(a, LANE - s, 1)
            if s + unit > LANE:
                a = jnp.where(lane < LANE - s, a, pltpu.roll(tiles[q + 1], LANE - s, 1))
        out.append(a)
    return out


def pack_gates(parts, unit, n_tiles):
    lane = lane_iota(parts[0].shape[0])
    rolled = [p if (k * unit) % LANE == 0 else pltpu.roll(p, (k * unit) % LANE, 1) for k, p in enumerate(parts)]
    tiles = []
    for q in range(n_tiles):
        val = jnp.zeros_like(parts[0])
        for k in range(4):
            a, b = k * unit - q * LANE, (k + 1) * unit - q * LANE
            if b > 0 and a < LANE:
                val = jnp.where((lane >= a) & (lane < b), rolled[k], val)
        tiles.append(val)
    return jnp.concatenate(tiles, axis=1)


def recur_kernel(C, R, T, B, U,
                 x_ref, wx1_ref, wh1_ref, wx2_ref, wh2_ref, b1_ref, b2_ref, hi_ref, ci_ref, g_ref,
                 left_ref, dzn_ref, gb_ref,
                 wx1, wh1, wx2, wh2, brow, pm, stage, xstage, wf, wt, wc1, wc2, xsib, xs, xr, zs, zr, h0, hist1, hist2, sv, c_out, c_in, cst,
                 bias, gs, part, r1, r2, s1, s2, dzo, dza, gbacc, gbbuf, pxs, zscr, dcs, d1, hspare, ins,
                 ws, wr, sbs, sbr, xss, xrs, zss, zrs, h0s, h0r, css, crs, h1s, h1r, h2s, h2r,
                 b1s, b1r, b2s, b2r, dzs, dzr, gbs, gbr):
    N = C * R
    CHIPS = R // 2
    unit = U // N
    rows = U // R
    cols = 4 * U // C
    ncol = 4 * unit
    npad = stage.shape[-1]
    c = lax.axis_index('col')
    r = lax.axis_index('row')
    me = c * R + r
    chip, core = r // 2, lax.rem(r, 2)
    sib = {'col': c, 'row': chip * 2 + 1 - core}
    my_s = lax.rem(r * unit, LANE)
    group = unit * R
    gw = -(-group // LANE) * LANE
    ring = lambda o, n: min(o, n - o)
    far_y = sorted(range(C), key=lambda o: -ring(o, C))
    far_row = sorted(((dx, dk) for dx in range(CHIPS) for dk in range(2)), key=lambda o: -ring(o[0], CHIPS))

    def col_at(dy):
        return lax.rem(c + dy, C)

    def row_at(dx, dk):
        return 2 * lax.rem(chip + dx, CHIPS) + lax.rem(core + dk, 2)

    peers = [(dy, dx, dk) for dy in range(C) for dx, dk in far_row if (dy, dx, dk) != (0, 0, 0)]
    peers.sort(key=lambda o: -(ring(o[0], C) + ring(o[1], CHIPS)))

    loads = [pltpu.make_async_copy(a, b, ins.at[i]) for i, (a, b) in
             enumerate(((wh1_ref, wh1), (wx1_ref, wx1), (wh2_ref, wh2), (wx2_ref, wx2)))]
    for load in loads:
        load.start()

    def dev(p):
        return {'col': p // R, 'row': lax.rem(p, R)}

    def row_dev(p):
        return {'col': c, 'row': p}

    bar = pltpu.get_barrier_semaphore()
    for k in range(1, N):
        pl.semaphore_signal(bar, inc=1, device_id=dev(lax.rem(me + k, N)), device_id_type=MESH)

    def start(src, dst, ss, rs, did):
        pltpu.make_async_remote_copy(src_ref=src, dst_ref=dst, send_sem=ss, recv_sem=rs, device_id=did, device_id_type=MESH).start()

    def wait(ref, sem):
        pltpu.make_async_copy(ref, ref, sem).wait()

    def win(p):
        return pl.multiple_of(jnp.minimum((p * ncol) // LANE * LANE, cols - WIN), LANE)

    kk = lax.broadcasted_iota(jnp.int32, (WIN, npad), 0)
    nn = lax.broadcasted_iota(jnp.int32, (WIN, npad), 1)
    gate = (nn >= unit).astype(jnp.int32) + (nn >= 2 * unit).astype(jnp.int32) + (nn >= 3 * unit).astype(jnp.int32)
    target = jnp.where(nn < ncol, 4 * (nn - unit * gate) + gate, -cols) - kk

    def regroup(w, p):
        return dot(w[:, pl.ds(win(p), WIN)], pm[p]).astype(BF16)

    def row_block(p):
        return pl.ds(pl.multiple_of(p * rows, 16), rows)

    def make_pm(p, _):
        pm[p] = jnp.where(target == win(p) - p * ncol, 1.0, 0.0).astype(BF16)
        return 0

    h0[r] = jnp.concatenate([hi_ref[...], jnp.zeros((2, B, npad - rows), F32)], axis=2).astype(BF16)
    lax.fori_loop(0, R, make_pm, 0)
    pl.semaphore_wait(bar, N - 1)
    start(x_ref, xsib, sbs.at[0], sbr.at[0], sib)
    for dx, dk in far_row:
        if (dx, dk) != (0, 0):
            start(h0.at[r], h0.at[r], h0s, h0r, row_dev(row_at(dx, dk)))
    loads[0].wait()

    def send_h1(k, _):
        p = lax.rem(r + R // 2 + k, R)
        stage[0, p] = regroup(wh1, p)

        @pl.when(p != r)
        def _():
            start(stage.at[0, p], wf.at[0, row_block(r)], ws.at[0], wr.at[0], row_dev(p))
        return 0

    lax.fori_loop(0, R, send_h1, 0)
    wf[0, row_block(r)] = stage[0, r]

    def send_h2(cut):
        lo, hi = W2_CUTS[cut], W2_CUTS[cut + 1]
        for dx, dk in far_row:
            if (dx, dk) != (0, 0):
                p = row_at(dx, dk)
                start(stage.at[1, p, pl.ds(lo, hi - lo)], wf.at[1, pl.ds(pl.multiple_of(r * rows + lo, 16), hi - lo)],
                      ws.at[1], wr.at[1], row_dev(p))

    owner = r * (N // R) + c
    ci = jnp.concatenate([ci_ref[...].reshape(2 * B, rows), jnp.zeros((2 * B, npad - rows), F32)], axis=1)
    lane2 = lane_iota(2 * B)
    for j in range(C):
        q, s = divmod(j * unit, LANE)
        v = ci[:, q * LANE:(q + 1) * LANE]
        if s:
            v = pltpu.roll(v, LANE - s, 1)
            if s + unit > LANE:
                v = jnp.where(lane2 < LANE - s, v, pltpu.roll(ci[:, (q + 1) * LANE:(q + 2) * LANE], LANE - s, 1))
        v = jnp.where(lane2 < unit, v, 0.0).reshape(2, B, LANE)

        @pl.when(c == j)
        def _():
            c_out[...] = v

    @pl.when(owner != me)
    def _():
        start(c_out, c_in, css, crs, dev(owner))

    @pl.when(owner == me)
    def _():
        c_in[...] = c_out[...]

    def trade1(j, _):
        mine, other = 2 * j + core, 2 * j + 1 - core
        wc1[j, row_block(core)] = regroup(wx1, mine)
        xstage[j] = regroup(wx1, other)
        start(xstage.at[j], wc1.at[j, row_block(core)], sbs.at[1], sbr.at[1], sib)
        return 0

    loads[1].wait()
    lax.fori_loop(0, CHIPS, trade1, 0)
    loads[2].wait()

    def stage_h2(p, _):
        stage[1, p] = regroup(wh2, p)
        return 0

    lax.fori_loop(0, R, stage_h2, 0)
    wait(xsib, sbr.at[0])
    wait(xstage, sbr.at[1])

    def flat(v):
        return v.astype(F32).reshape(T * B, rows).astype(BF16)

    def xproj(j, _):
        v = dot(flat(x_ref[...]), wc1[j, row_block(core)]) + dot(flat(xsib[...]), wc1[j, row_block(1 - core)])
        xs[j] = v.reshape(T, B, npad)
        return 0

    lax.fori_loop(0, CHIPS, xproj, 0)

    def send_x(cut):
        ts = pl.ds(X_CUTS[cut], X_CUTS[cut + 1] - X_CUTS[cut])
        for k in (2, 1, 3):
            j = lax.rem(chip + k, CHIPS)
            start(xs.at[j, ts], xr.at[chip, ts], xss.at[cut], xrs.at[cut], row_dev(2 * j + core))

    def wait_x(cut, sems):
        wait(xs.at[pl.ds(0, CHIPS - 1), pl.ds(X_CUTS[cut], X_CUTS[cut + 1] - X_CUTS[cut])], sems.at[cut])

    send_x(0)
    xr[chip] = xs[chip]
    send_h2(0)
    wf[1, row_block(r)] = stage[1, r]
    loads[3].wait()

    def trade2(j, _):
        mine, other = 2 * j + core, 2 * j + 1 - core
        blk = regroup(wx2, mine)
        stage[2, mine] = blk
        wc2[j, row_block(core)] = blk
        stage[2, other] = regroup(wx2, other)
        start(stage.at[2, other], wc2.at[j, row_block(core)], sbs.at[2], sbr.at[2], sib)
        return 0

    lax.fori_loop(0, CHIPS, trade2, 0)
    wf[2, row_block(r)] = stage[2, r]

    for l, ref in enumerate((b1_ref, b2_ref)):
        brow[...] = jnp.broadcast_to(ref[...].reshape(1, cols), (B, cols))
        b = brow[:, pl.ds(win(r), WIN)]
        bias[l] = by_thirds(b, lambda v: dot(v, pm[r]))
    g_w = g_ref.shape[2]
    sel_k = lax.broadcasted_iota(jnp.int32, (g_w, LANE), 0)
    sel_n = lax.broadcasted_iota(jnp.int32, (g_w, LANE), 1)
    sel = jnp.where((sel_k == sel_n + r * unit) & (sel_n < unit), 1.0, 0.0).astype(BF16)
    gs[...] = dot(g_ref[...].astype(F32).reshape(T * B, g_w).astype(BF16), sel).reshape(T, B, LANE)

    def transpose_w(w):
        eye = (lax.broadcasted_iota(jnp.int32, (npad, npad), 0) == lax.broadcasted_iota(jnp.int32, (npad, npad), 1))
        eye = jnp.where(eye, 1.0, 0.0).astype(BF16)

        def body(k, _):
            for off in range(0, group, 256):
                n = min(256, group - off)
                v = dot_t(eye, wf[w, pl.ds(pl.multiple_of(k * group + off, 16), n)]).astype(BF16)
                if off + n == group and gw > group:
                    v = jnp.concatenate([v, jnp.zeros((npad, gw - group), BF16)], axis=1)
                wt[w, :, pl.ds(pl.multiple_of(k * gw + off, LANE), v.shape[1])] = v
            return 0
        lax.fori_loop(0, C, body, 0)

    def cell(layer, t, z):
        zi, zf, zg, zo = split_gates(z, unit)
        gi, gf, gg, go = jax.nn.sigmoid(zi), jax.nn.sigmoid(zf), jnp.tanh(zg), jax.nn.sigmoid(zo)
        c_prev = cst[layer]
        c_new = gf * c_prev + gi * gg
        tc = jnp.tanh(c_new)
        cst[layer] = c_new
        for k, v in enumerate((gi, gf, gg, go, c_prev, tc)):
            sv[layer, t, k] = v
        return pltpu.roll(go * tc, my_s, 1).astype(BF16)

    def bcast(hist, t, ss, rs):
        for dy, dx, dk in peers:
            start(hist.at[t, c, r], hist.at[t, c, r], ss.at[t], rs.at[t, c], {'col': col_at(dy), 'row': row_at(dx, dk)})

    def group_h(hist, t, cs):
        return join([(unit * d, hist[t, cs, d].astype(F32)) for d in range(R)], gw)[:, :group].astype(BF16)

    def h_times(hist, t, rs, w):
        z = jnp.zeros((B, npad), F32)
        for dy in far_y[::-1]:
            cs = col_at(dy)
            wait(hist.at[t, cs, pl.ds(0, R if dy else R - 1)], rs.at[t, cs])
            z = z + dot(group_h(hist, t, cs), wf[w, pl.ds(pl.multiple_of(cs * group, 16), group)])
        return z

    def from_h0(layer):
        v = jnp.zeros((B, npad), F32)
        for p in range(R):
            v = v + dot(h0[p, layer][:, :rows], wf[layer, p * rows:(p + 1) * rows])
        return v

    def total(ref, t):
        return (ref[0, t] + ref[1, t]) + (ref[2, t] + ref[3, t])

    def partial_z2(t):
        h = group_h(hist1, t, chip)
        for j in range(CHIPS):
            zs[j, t] = dot(h, wc2[j])
        for k in (2, 1, 3):
            j = lax.rem(chip + k, CHIPS)
            start(zs.at[j, t], zr.at[chip, t], zss.at[t], zrs.at[t], row_dev(2 * j + core))
        zr[chip, t] = zs[chip, t]

    @pl.when(owner != me)
    def _():
        wait(c_in, crs)
    cst[...] = c_in[...]
    wait(h0.at[pl.ds(0, R - 1)], h0r)
    wait_x(0, xrs)
    wait(stage.at[0, pl.ds(0, R - 1)], wr.at[0])
    hist1[0, c, r] = cell(0, 0, total(xr, 0) + bias[0] + from_h0(0))
    bcast(hist1, 0, h1s, h1r)
    send_h2(1)
    wait(xstage, sbr.at[2])

    n_pieces = rows // WROWS

    def fwd(s, _):
        for cut in range(1, len(X_CUTS) - 1):
            @pl.when(s == X_CUTS[cut] - 1)
            def _():
                wait_x(cut, xrs)

        @pl.when(s < T - 1)
        def _():
            hist1[s + 1, c, r] = cell(0, s + 1, total(xr, s + 1) + bias[0] + h_times(hist1, s, h1r, 0))
            bcast(hist1, s + 1, h1s, h1r)

        @pl.when(s == T - 1)
        def _():
            for dy in range(C):
                cs = col_at(dy)
                wait(hist1.at[s, cs, pl.ds(0, R if dy else R - 1)], h1r.at[s, cs])

        @pl.when(s < T)
        def _():
            partial_z2(s)

        @pl.when(s == 0)
        def _():
            send_h2(2)

        @pl.when(s == 1)
        def _():
            wait(stage.at[1, pl.ds(0, R - 1)], wr.at[1])
            zscr[...] = from_h0(1)

        @pl.when(s > 1)
        def _():
            zscr[...] = h_times(hist2, s - 2, h2r, 1)

        @pl.when(s > 0)
        def _():
            wait(zs.at[pl.ds(0, CHIPS - 1), s - 1], zrs.at[s - 1])
            hist2[s - 1, c, r] = cell(1, s - 1, total(zr, s - 1) + bias[1] + zscr[...])

            @pl.when(s < T)
            def _():
                bcast(hist2, s - 1, h2s, h2r)

        for cut in range(1, len(X_CUTS) - 1):
            @pl.when(s == X_SEND[cut])
            def _():
                send_x(cut)

        @pl.when((s >= 3) & (s < 3 + n_pieces))
        def _():
            piece = pl.ds(pl.multiple_of((s - 3) * WROWS, WROWS), WROWS)
            dest = pl.ds(pl.multiple_of(r * rows + (s - 3) * WROWS, WROWS), WROWS)
            for k in range(1, R):
                p = lax.rem(r + k, R)
                start(stage.at[2, p, piece], wf.at[2, dest], ws.at[2], wr.at[2], row_dev(p))

        @pl.when(s == 2)
        def _():
            transpose_w(0)

        @pl.when(s == 4)
        def _():
            transpose_w(1)

        @pl.when(s == T - 1)
        def _():
            wait(stage.at[2, pl.ds(0, R - 1)], wr.at[2])
            transpose_w(2)
        return 0

    lax.fori_loop(0, T + 1, fwd, 0)

    gbacc[...] = jnp.zeros_like(gbacc)
    dcs[...] = jnp.zeros_like(dcs)

    def cell_grad(layer, t, dh):
        gi, gf, gg, go, c_prev, tc = [sv[layer, t, k] for k in range(6)]
        dc = dcs[layer] + dh * go * (1.0 - tc * tc)
        dz = (dc * gg * gi * (1.0 - gi), dc * c_prev * gf * (1.0 - gf), dc * gi * (1.0 - gg * gg), dh * tc * go * (1.0 - go))
        dcs[layer] = dc * gf
        for k in range(4):
            gbacc[layer, k] += dz[k]
        packed = pack_gates(dz, unit, npad // LANE).astype(BF16)
        dzo[layer, t] = packed
        return packed

    lane_b = lane_iota(B)

    def scatter(term, sbuf, rbuf, t, ss, rs):
        for i, dy in enumerate(far_y):
            cs = col_at(dy)
            p = term(pl.ds(pl.multiple_of(cs * gw, LANE), gw))
            tiles = [p[:, q * LANE:(q + 1) * LANE] for q in range(gw // LANE)]
            for d in range(R):
                q, off = divmod(d * unit, LANE)
                v = tiles[q]
                if off + unit > LANE:
                    v = jnp.where(lane_b >= off, v, tiles[q + 1])
                sbuf[t, i, d] = v
            for dx, dk in far_row:
                if (dy, dx, dk) != (0, 0, 0):
                    p = row_at(dx, dk)
                    start(sbuf.at[t, i, p], rbuf.at[t, me], ss.at[t], rs.at[t], {'col': cs, 'row': p})
            if dy == 0:
                rbuf[t, me] = sbuf[t, i, r]

    def reduced(rbuf, t, rs):
        wait(rbuf.at[t, pl.ds(0, N - 1)], rs.at[t])
        vals = [rbuf[t, d] for d in range(N)]
        while len(vals) > 1:
            vals = [a + b for a, b in zip(vals[::2], vals[1::2])]
        return pltpu.roll(vals[0], lax.rem(LANE - my_s, LANE), 1)

    order = pm.at[0, pl.ds(0, npad)]

    def send_dz(layer, t):
        @pl.when(lax.rem(t, CH) == 0)
        def _():
            ts = pl.ds(t, CH)
            v = dzo[layer, ts].astype(F32).reshape(CH * B, npad).astype(BF16)
            dza[layer, r, ts] = dot_t(v, order[...]).reshape(CH, B, npad).astype(BF16)
            for k in range(1, R):
                start(dza.at[layer, r, ts], dza.at[layer, r, ts], dzs.at[layer, t // CH], dzr.at[layer, t // CH],
                      row_dev(lax.rem(r + k, R)))

    def blocks_joined(get):
        segs = []
        for p in range(R):
            v = get(p)
            for a in range(npad // LANE):
                tile = v[:, a * LANE:(a + 1) * LANE]
                s = (p * ncol) % LANE
                segs.append((p * ncol + a * LANE, pltpu.roll(tile, s, 1) if s else tile))
        return join(segs, cols)

    def place_dz(q):
        for layer in range(2):
            wait(dza.at[layer, pl.ds(0, R - 1), pl.ds(0, CH)], dzr.at[layer, q])
            v = blocks_joined(lambda p: dza[layer, p, pl.ds(q * CH, CH)].astype(F32).reshape(CH * B, npad))
            dzn_ref[layer, pl.ds(pl.multiple_of(q * (CH * B), CH * B), CH * B)] = v.astype(BF16)

    shift = core * ((LANE - rows % LANE) % LANE)
    per = R // 2

    def local_rows(hist, count):
        segs = [(unit * d, pltpu.roll(hist[pl.ds(0, count), chip, per * core + d].astype(F32).reshape(count * B, LANE), shift, 1))
                for d in range(per)]
        return join(segs, npad)

    def put_left(i, v):
        for a in range(npad // LANE):
            left_ref[i, a * LANE:(a + 1) * LANE] = v[:, a * LANE:(a + 1) * LANE].T.astype(BF16)

    def wide(v):
        return jnp.concatenate([v, jnp.zeros((v.shape[0], npad - rows), F32)], axis=1)

    def bwd(s, _):
        t = T - 1 - s
        part[...] = gs[t]

        @pl.when(s > 0)
        def _():
            part[...] += reduced(r2, t, b2r)

        dz2 = cell_grad(1, t, part[...])

        @pl.when(t > 0)
        def _():
            scatter(lambda n: dot(dz2, wt[1, :, n]), s2, r2, t - 1, b2s, b2r)

        pxs[...] = dot(dz2, wt[2])
        send_dz(1, t)

        @pl.when(s == 0)
        def _():
            d1[...] = jnp.zeros_like(d1)

        @pl.when(s > 0)
        def _():
            d1[...] = cell_grad(0, t + 1, reduced(r1, t + 1, b1r))

        scatter(lambda n: dot(d1[...], wt[0, :, n]) + pxs[:, n], s1, r1, t, b1s, b1r)

        @pl.when(s > 0)
        def _():
            send_dz(0, t + 1)

        @pl.when((s >= CH + 2) & (lax.rem(s, CH) == 2))
        def _():
            place_dz(T // CH - 1 - (s - CH - 2) // CH)

        @pl.when(s == 1)
        def _():
            put_left(0, wide(x_ref[...].astype(F32).reshape(T * B, rows)))

        @pl.when(s == 2)
        def _():
            h1_rows = local_rows(hist1, T)
            put_left(2, h1_rows)
            first = h0[r, 0].astype(F32)
            put_left(1, jnp.concatenate([first, h1_rows[:(T - 1) * B]], axis=0))

        @pl.when(s == 3)
        def _():
            put_left(3, jnp.concatenate([h0[r, 1].astype(F32), local_rows(hist2, T - 1)], axis=0))
        return 0

    lax.fori_loop(0, T, bwd, 0)
    cell_grad(0, 0, reduced(r1, 0, b1r))
    send_dz(0, 0)

    sub = lax.broadcasted_iota(jnp.int32, (8, LANE), 0)
    packed = []
    for k in range(4):
        b0 = jnp.sum(gbacc[0, k], axis=0, keepdims=True)
        b1 = jnp.sum(gbacc[1, k], axis=0, keepdims=True)
        packed.append(jnp.where(sub == 0, jnp.broadcast_to(b0, (8, LANE)), jnp.broadcast_to(b1, (8, LANE))))
    gbbuf[r] = by_thirds(pack_gates(packed, unit, npad // LANE), lambda v: dot_t(v, order[...]))
    for k in range(1, R):
        start(gbbuf.at[r], gbbuf.at[r], gbs, gbr, row_dev(lax.rem(r + k, R)))

    wait(x_ref, sbs.at[0])
    wait(xstage, sbs.at[1])
    wait(xstage, sbs.at[2])
    for w in range(3):
        wait(stage.at[w, pl.ds(0, R - 1)], ws.at[w])
    wait(h0.at[pl.ds(0, R - 1)], h0s)
    for cut in range(len(X_CUTS) - 1):
        wait_x(cut, xss)

    @pl.when(owner != me)
    def _():
        wait(c_in, css)

    hflat = hspare.at[pl.ds(0, N - 1)]

    def drain(t, _):
        wait(r1.at[0, pl.ds(0, N - 1)], b1s.at[t])
        wait(zs.at[pl.ds(0, CHIPS - 1), t], zss.at[t])
        wait(hflat, h1s.at[t])

        @pl.when(t < T - 1)
        def _():
            wait(r1.at[0, pl.ds(0, N - 1)], b2s.at[t])
            wait(hflat, h2s.at[t])
        return 0

    lax.fori_loop(0, T, drain, 0)
    place_dz(0)
    wait(gbbuf.at[pl.ds(0, R - 1)], gbr)
    gb_ref[...] = blocks_joined(lambda p: gbbuf[p])
    for layer in range(2):
        for q in range(T // CH):
            wait(dza.at[layer, pl.ds(0, R - 1), pl.ds(0, CH)], dzs.at[layer, q])
    wait(gbbuf.at[pl.ds(0, R - 1)], gbs)


def grad_kernel(left_ref, dzn_ref, gb_ref, gx1, gh1, gx2, gh2, gb1, gb2, buf, sems):
    rows = gx1.shape[0]
    step = rows // GROWS
    copies = []
    for i in range(GROWS):
        for k, (out, layer) in enumerate(((gx1, 0), (gh1, 0), (gx2, 1), (gh2, 1))):
            lo = i * step
            buf[k, lo:lo + step] = dot(left_ref[k, lo:lo + step], dzn_ref[layer])
            copies.append(pltpu.make_async_copy(buf.at[k, pl.ds(lo, step)], out.at[pl.ds(lo, step)], sems.at[k, i]))
            copies[-1].start()
    gb1[...] = gb_ref[0]
    gb2[...] = gb_ref[1]
    for copy in copies:
        copy.wait()


def solution(mesh):
    C, R = mesh.shape['col'], mesh.shape['row']
    N = C * R
    seq_spec = P(None, 'data', 'row')
    w_spec = P('row', 'col')
    bias_spec = P('col')
    g_spec = P(None, 'data', 'col')
    grad_spec = P(('data', 'row'), 'col')
    gbias_spec = P(('data', 'col'))

    def local_grads(seq_in, w_x1, w_h1, w_x2, w_h2, bias_1, bias_2, h_init, c_init, g_out):
        T, B, rows = seq_in.shape
        U = rows * R
        cols = w_x1.shape[1]
        unit = U // N
        npad = -(-4 * unit // LANE) * LANE
        chips = R // 2
        gw = -(-unit * R // LANE) * LANE
        vm = pl.BlockSpec(memory_space=pltpu.VMEM)
        dma = pltpu.SemaphoreType.DMA
        V = pltpu.VMEM
        left, dzn, gb = pl.pallas_call(
            functools.partial(recur_kernel, C, R, T, B, U),
            name='recur',
            out_shape=(jax.ShapeDtypeStruct((4, npad, T * B), BF16), jax.ShapeDtypeStruct((2, T * B, cols), BF16),
                       jax.ShapeDtypeStruct((8, cols), F32)),
            in_specs=[vm] + [pl.BlockSpec(memory_space=pl.ANY)] * 4 + [vm] * 5,
            out_specs=(vm, vm, vm),
            scratch_shapes=[
                V((rows, cols), BF16), V((rows, cols), BF16), V((rows, cols), BF16), V((rows, cols), BF16),
                V((B, cols), F32),
                V((R, WIN, npad), BF16),
                V((3, R, rows, npad), BF16),
                V((chips, rows, npad), BF16),
                V((3, U, npad), BF16),
                V((3, npad, C * gw), BF16),
                V((chips, 2 * rows, npad), BF16),
                V((chips, 2 * rows, npad), BF16),
                V((T, B, rows), BF16),
                V((chips, T, B, npad), F32),
                V((chips, T, B, npad), F32),
                V((chips, T, B, npad), F32),
                V((chips, T, B, npad), F32),
                V((R, 2, B, npad), BF16),
                V((T, C, R, B, LANE), BF16),
                V((T, C, R, B, LANE), BF16),
                V((2, T, 6, B, LANE), F32),
                V((2, B, LANE), F32),
                V((2, B, LANE), F32),
                V((2, B, LANE), F32),
                V((2, B, npad), F32),
                V((T, B, LANE), F32),
                V((B, LANE), F32),
                V((T, N, B, LANE), F32),
                V((T, N, B, LANE), F32),
                V((T, C, R, B, LANE), F32),
                V((T, C, R, B, LANE), F32),
                V((2, T, B, npad), BF16),
                V((2, R, T, B, npad), BF16),
                V((2, 4, B, LANE), F32),
                V((R, 8, npad), F32),
                V((B, C * gw), F32),
                V((B, npad), F32),
                V((2, B, LANE), F32),
                V((B, npad), BF16),
                V((N, B, LANE), BF16),
                dma((4,)),
                dma((3,)), dma((3,)), dma((3,)), dma((3,)), dma((len(X_CUTS) - 1,)), dma((len(X_CUTS) - 1,)), dma((T,)), dma((T,)),
                dma, dma, dma, dma,
                dma((T,)), dma((T, C)), dma((T,)), dma((T, C)),
                dma((T,)), dma((T,)), dma((T,)), dma((T,)),
                dma((2, T // CH)), dma((2, T // CH)), dma, dma,
            ],
            compiler_params=pltpu.CompilerParams(collective_id=0, has_side_effects=True, vmem_limit_bytes=63 * 1024 * 1024),
        )(seq_in, w_x1, w_h1, w_x2, w_h2, bias_1, bias_2, h_init, c_init, g_out)

        out = jax.ShapeDtypeStruct((rows, cols), F32)
        bout = jax.ShapeDtypeStruct((cols,), F32)
        hbm = pl.BlockSpec(memory_space=pl.ANY)
        return tuple(pl.pallas_call(
            grad_kernel,
            name='grads',
            out_shape=(out,) * 4 + (bout,) * 2,
            in_specs=[vm] * 3,
            out_specs=(hbm,) * 4 + (vm,) * 2,
            scratch_shapes=[V((4, rows, cols), F32), dma((4, GROWS))],
            compiler_params=pltpu.CompilerParams(vmem_limit_bytes=40 * 1024 * 1024),
        )(left, dzn, gb))

    return jax.shard_map(local_grads, mesh=mesh,
                         in_specs=(seq_spec, w_spec, w_spec, w_spec, w_spec, bias_spec, bias_spec, seq_spec, seq_spec, g_spec),
                         out_specs=(grad_spec, grad_spec, grad_spec, grad_spec, gbias_spec, gbias_spec),
                         check_vma=False)
```

time: 312 us -> 260 us (0.83)
  Pallas kernels: 302 us -> 256 us
  local copies, waits for them, and re-layouts: 7.43 us -> 3.24 us
    pallas_call x1, Pallas kernels: 292 us -> 249 us  [local_grads(): pl.pallas_call(functools.partial(recur_kernel, C, R, T, B, U), name='recu...]
    pallas_call x1, Pallas kernels: 10.2 us -> 6.61 us  [local_grads(): pl.pallas_call(grad_kernel, name='grads', out_shape=(out,) * 4 + (bout,)...]
    unnamed x2 -> x6, local copies, waits for them, and re-layouts: 0.01 us -> 3.24 us
where the time goes in v2:
time: 260 us
  Pallas kernels  256 us (98%)
  local copies, waits for them, and re-layouts  3.24 us (1%)
    pallas_call x1, Pallas kernels, local_grads(): pl.pallas_call(functools.partial(recur_kernel, C, R, T, B, U), name='recu...  249 us
    pallas_call x1, Pallas kernels, local_grads(): pl.pallas_call(grad_kernel, name='grads', out_shape=(out,) * 4 + (bout,)...  6.61 us

profile of v2, /device:TPU:97, one launch (start us, length us, event | category | flops | bytes accessed | tf_op | source)
XLA Modules:
  0.0 260.0 jit_solution(11359016933896838210)
XLA Ops:
  0.6 249.3 %recur.1 = (bf16[4,384,128]{2,1,0:T(8,128)(2,1)}, bf16[2,128,2816]{2,1,0:T(8,128)(2,1)}, f32[8,2816]{1,0:T(8,128)}) custom-call(bf16[16,8,352]{2,1,0:T(8,128)(2,1)} %x_ref.1, bf16[352,2816]{1,0:T(8,128)(2,1)} %wx1_ref.1, bf16[352,2816]{1,0:T(8,128)(2,1)} %wh1_ref.1, bf16[352,2816]{1,0:T(8,128)(2,1)} %wx2_ref.1, bf16[352,2816]{1,0:T(8,128)(2,1)} %wh2_ref.1, ...), custom_call_target="tpu_custom_call" | custom-call | tf_op jit(solution)/shard_map/recur/pallas_call | solution.py:646
  250.0 0.0 copy-start
  250.0 1.4 copy-done
  251.3 0.0 copy-start.1
  251.3 1.0 copy-done.1
  252.3 0.0 copy-start.2
  252.3 0.9 copy-done.2
  253.2 6.6 %grads.1 = (f32[352,2816]{1,0:T(8,128)}, f32[352,2816]{1,0:T(8,128)}, f32[352,2816]{1,0:T(8,128)}, f32[352,2816]{1,0:T(8,128)}, f32[2816]{0:T(1024)}, /*index=5*/f32[2816]{0:T(1024)}) custom-call(bf16[4,384,128]{2,1,0:T(8,128)(2,1)S(1)} %copy-done.1, bf16[2,128,2816]{2,1,0:T(8,128)(2,1)S(1)} %copy-done, f32[8,2816]{1,0:T(8,128)S(1)} %copy-done.2), custom_call_target="tpu_custom_call" | custom-call | tf_op jit(solution)/shard_map/grads/pallas_call | solution.py:704
Async XLA Ops:
  250.0 1.4 copy-start
  251.3 1.0 copy-start.1
  252.3 0.9 copy-start.2

commit v3 on v2

--- a/solution.py
+++ b/solution.py
@@ -13,11 +13,12 @@
 LANE = 128
 WIN = 512
 CH = 4
-X_CUTS = (0, 6, 9, 12, 16)
-X_SEND = (None, 2, 4, 6)
+X_CUTS = (0, 4, 8, 12, 16)
+X_SEND = (None, 1, 3, 5)
 W2_CUTS = (0, 128, 240, 352)
 GROWS = 4
 WROWS = 32
+W_FROM = 4
 
 
 def dot(a, b):
@@ -35,6 +36,13 @@
     mid = rest.astype(BF16)
     lo = (rest - mid.astype(F32)).astype(BF16)
     return ((f(hi) + f(mid)) + f(lo)) * 4.0
+
+
+def loop(n, body):
+    def step(i, carry):
+        body(i, carry)
+        return carry
+    lax.fori_loop(0, n, step, 0)
 
 
 def lane_iota(rows):
@@ -86,9 +94,10 @@
 
 def recur_kernel(C, R, T, B, U,
                  x_ref, wx1_ref, wh1_ref, wx2_ref, wh2_ref, b1_ref, b2_ref, hi_ref, ci_ref, g_ref,
+                 left_out, dzn_out, gb_out,
                  left_ref, dzn_ref, gb_ref,
                  wx1, wh1, wx2, wh2, brow, pm, stage, xstage, wf, wt, wc1, wc2, xsib, xs, xr, zs, zr, h0, hist1, hist2, sv, c_out, c_in, cst,
-                 bias, gs, part, r1, r2, s1, s2, dzo, dza, gbacc, gbbuf, pxs, zscr, dcs, d1, hspare, ins,
+                 bias, gs, part, r1, r2, s1, s2, dzo, dza, gbacc, gbbuf, pxs, zscr, dcs, d1, hspare, zh, zhr, ins, outs, zhs,
                  ws, wr, sbs, sbr, xss, xrs, zss, zrs, h0s, h0r, css, crs, h1s, h1r, h2s, h2r,
                  b1s, b1r, b2s, b2r, dzs, dzr, gbs, gbr):
     N = C * R
@@ -117,13 +126,15 @@
         return 2 * lax.rem(chip + dx, CHIPS) + lax.rem(core + dk, 2)
 
     peers = [(dy, dx, dk) for dy in range(C) for dx, dk in far_row if (dy, dx, dk) != (0, 0, 0)]
-    peers.sort(key=lambda o: -(ring(o[0], C) + ring(o[1], CHIPS)))
+    peers.sort(key=lambda o: (not (o[0] and o[1]), -(ring(o[0], C) + ring(o[1], CHIPS))))
 
     loads = [pltpu.make_async_copy(a, b, ins.at[i]) for i, (a, b) in
              enumerate(((wh1_ref, wh1), (wx1_ref, wx1), (wh2_ref, wh2), (wx2_ref, wx2)))]
     for load in loads:
         load.start()
 
+    others_r, others_n, others_c = (pl.ds(0, n - 1) for n in (R, N, CHIPS))
+
     def dev(p):
         return {'col': p // R, 'row': lax.rem(p, R)}
 
@@ -156,10 +167,9 @@
 
     def make_pm(p, _):
         pm[p] = jnp.where(target == win(p) - p * ncol, 1.0, 0.0).astype(BF16)
-        return 0
 
     h0[r] = jnp.concatenate([hi_ref[...], jnp.zeros((2, B, npad - rows), F32)], axis=2).astype(BF16)
-    lax.fori_loop(0, R, make_pm, 0)
+    loop(R, make_pm)
     pl.semaphore_wait(bar, N - 1)
     start(x_ref, xsib, sbs.at[0], sbr.at[0], sib)
     for dx, dk in far_row:
@@ -174,9 +184,8 @@
         @pl.when(p != r)
         def _():
             start(stage.at[0, p], wf.at[0, row_block(r)], ws.at[0], wr.at[0], row_dev(p))
-        return 0
-
-    lax.fori_loop(0, R, send_h1, 0)
+
+    loop(R, send_h1)
     wf[0, row_block(r)] = stage[0, r]
 
     def send_h2(cut):
@@ -216,17 +225,22 @@
         wc1[j, row_block(core)] = regroup(wx1, mine)
         xstage[j] = regroup(wx1, other)
         start(xstage.at[j], wc1.at[j, row_block(core)], sbs.at[1], sbr.at[1], sib)
-        return 0
 
     loads[1].wait()
-    lax.fori_loop(0, CHIPS, trade1, 0)
+    loop(CHIPS, trade1)
     loads[2].wait()
 
-    def stage_h2(p, _):
+    def stage_h2(k, _):
+        p = lax.rem(r + R // 2 + k, R)
         stage[1, p] = regroup(wh2, p)
-        return 0
-
-    lax.fori_loop(0, R, stage_h2, 0)
+        zh[p] = dot(h0[r, 1][:, :rows], stage[1, p])
+
+        @pl.when(p != r)
+        def _():
+            start(zh.at[p], zhr.at[r], zhs.at[0], zhs.at[1], row_dev(p))
+
+    loop(R, stage_h2)
+    zhr[r] = zh[r]
     wait(xsib, sbr.at[0])
     wait(xstage, sbr.at[1])
 
@@ -236,9 +250,8 @@
     def xproj(j, _):
         v = dot(flat(x_ref[...]), wc1[j, row_block(core)]) + dot(flat(xsib[...]), wc1[j, row_block(1 - core)])
         xs[j] = v.reshape(T, B, npad)
-        return 0
-
-    lax.fori_loop(0, CHIPS, xproj, 0)
+
+    loop(CHIPS, xproj)
 
     def send_x(cut):
         ts = pl.ds(X_CUTS[cut], X_CUTS[cut + 1] - X_CUTS[cut])
@@ -247,7 +260,7 @@
             start(xs.at[j, ts], xr.at[chip, ts], xss.at[cut], xrs.at[cut], row_dev(2 * j + core))
 
     def wait_x(cut, sems):
-        wait(xs.at[pl.ds(0, CHIPS - 1), pl.ds(X_CUTS[cut], X_CUTS[cut + 1] - X_CUTS[cut])], sems.at[cut])
+        wait(xs.at[others_c, pl.ds(X_CUTS[cut], X_CUTS[cut + 1] - X_CUTS[cut])], sems.at[cut])
 
     send_x(0)
     xr[chip] = xs[chip]
@@ -262,9 +275,8 @@
         wc2[j, row_block(core)] = blk
         stage[2, other] = regroup(wx2, other)
         start(stage.at[2, other], wc2.at[j, row_block(core)], sbs.at[2], sbr.at[2], sib)
-        return 0
-
-    lax.fori_loop(0, CHIPS, trade2, 0)
+
+    loop(CHIPS, trade2)
     wf[2, row_block(r)] = stage[2, r]
 
     for l, ref in enumerate((b1_ref, b2_ref)):
@@ -288,8 +300,7 @@
                 if off + n == group and gw > group:
                     v = jnp.concatenate([v, jnp.zeros((npad, gw - group), BF16)], axis=1)
                 wt[w, :, pl.ds(pl.multiple_of(k * gw + off, LANE), v.shape[1])] = v
-            return 0
-        lax.fori_loop(0, C, body, 0)
+        loop(C, body)
 
     def cell(layer, t, z):
         zi, zf, zg, zo = split_gates(z, unit)
@@ -310,11 +321,15 @@
         return join([(unit * d, hist[t, cs, d].astype(F32)) for d in range(R)], gw)[:, :group].astype(BF16)
 
     def h_times(hist, t, rs, w):
-        z = jnp.zeros((B, npad), F32)
-        for dy in far_y[::-1]:
-            cs = col_at(dy)
-            wait(hist.at[t, cs, pl.ds(0, R if dy else R - 1)], rs.at[t, cs])
-            z = z + dot(group_h(hist, t, cs), wf[w, pl.ds(pl.multiple_of(cs * group, 16), group)])
+        def term(cs):
+            return dot(group_h(hist, t, cs), wf[w, pl.ds(pl.multiple_of(cs * group, 16), group)])
+
+        wait(hist.at[t, c, others_r], rs.at[t, c])
+        z = term(c)
+        for dy in range(1, C):
+            wait(hist.at[t, col_at(dy), pl.ds(0, R)], rs.at[t, col_at(dy)])
+        for dy in range(1, C):
+            z = z + term(col_at(dy))
         return z
 
     def from_h0(layer):
@@ -339,9 +354,9 @@
     def _():
         wait(c_in, crs)
     cst[...] = c_in[...]
-    wait(h0.at[pl.ds(0, R - 1)], h0r)
+    wait(h0.at[others_r], h0r)
     wait_x(0, xrs)
-    wait(stage.at[0, pl.ds(0, R - 1)], wr.at[0])
+    wait(stage.at[0, others_r], wr.at[0])
     hist1[0, c, r] = cell(0, 0, total(xr, 0) + bias[0] + from_h0(0))
     bcast(hist1, 0, h1s, h1r)
     send_h2(1)
@@ -376,8 +391,15 @@
 
         @pl.when(s == 1)
         def _():
-            wait(stage.at[1, pl.ds(0, R - 1)], wr.at[1])
-            zscr[...] = from_h0(1)
+            wait(zh.at[others_r], zhs.at[1])
+            v = zhr[0]
+            for p in range(1, R):
+                v = v + zhr[p]
+            zscr[...] = v
+
+        @pl.when(s == 2)
+        def _():
+            wait(stage.at[1, others_r], wr.at[1])
 
         @pl.when(s > 1)
         def _():
@@ -385,7 +407,7 @@
 
         @pl.when(s > 0)
         def _():
-            wait(zs.at[pl.ds(0, CHIPS - 1), s - 1], zrs.at[s - 1])
+            wait(zs.at[others_c, s - 1], zrs.at[s - 1])
             hist2[s - 1, c, r] = cell(1, s - 1, total(zr, s - 1) + bias[1] + zscr[...])
 
             @pl.when(s < T)
@@ -397,10 +419,10 @@
             def _():
                 send_x(cut)
 
-        @pl.when((s >= 3) & (s < 3 + n_pieces))
-        def _():
-            piece = pl.ds(pl.multiple_of((s - 3) * WROWS, WROWS), WROWS)
-            dest = pl.ds(pl.multiple_of(r * rows + (s - 3) * WROWS, WROWS), WROWS)
+        @pl.when((s >= W_FROM) & (s < W_FROM + n_pieces))
+        def _():
+            piece = pl.ds(pl.multiple_of((s - W_FROM) * WROWS, WROWS), WROWS)
+            dest = pl.ds(pl.multiple_of(r * rows + (s - W_FROM) * WROWS, WROWS), WROWS)
             for k in range(1, R):
                 p = lax.rem(r + k, R)
                 start(stage.at[2, p, piece], wf.at[2, dest], ws.at[2], wr.at[2], row_dev(p))
@@ -415,11 +437,10 @@
 
         @pl.when(s == T - 1)
         def _():
-            wait(stage.at[2, pl.ds(0, R - 1)], wr.at[2])
+            wait(stage.at[2, others_r], wr.at[2])
             transpose_w(2)
-        return 0
-
-    lax.fori_loop(0, T + 1, fwd, 0)
+
+    loop(T + 1, fwd)
 
     gbacc[...] = jnp.zeros_like(gbacc)
     dcs[...] = jnp.zeros_like(dcs)
@@ -448,15 +469,16 @@
                 if off + unit > LANE:
                     v = jnp.where(lane_b >= off, v, tiles[q + 1])
                 sbuf[t, i, d] = v
-            for dx, dk in far_row:
-                if (dy, dx, dk) != (0, 0, 0):
+            late = [] if dy else [(j, far_y[j], 0, dk) for j in range(C - 1) for dk in range(2)]
+            for j, y, dx, dk in [(i, dy, dx, dk) for dx, dk in far_row if dx or not dy] + late:
+                if (y, dx, dk) != (0, 0, 0):
                     p = row_at(dx, dk)
-                    start(sbuf.at[t, i, p], rbuf.at[t, me], ss.at[t], rs.at[t], {'col': cs, 'row': p})
+                    start(sbuf.at[t, j, p], rbuf.at[t, me], ss.at[t], rs.at[t], {'col': col_at(y), 'row': p})
             if dy == 0:
                 rbuf[t, me] = sbuf[t, i, r]
 
     def reduced(rbuf, t, rs):
-        wait(rbuf.at[t, pl.ds(0, N - 1)], rs.at[t])
+        wait(rbuf.at[t, others_n], rs.at[t])
         vals = [rbuf[t, d] for d in range(N)]
         while len(vals) > 1:
             vals = [a + b for a, b in zip(vals[::2], vals[1::2])]
@@ -484,11 +506,16 @@
                 segs.append((p * ncol + a * LANE, pltpu.roll(tile, s, 1) if s else tile))
         return join(segs, cols)
 
+    def chunk_like(layer):
+        return dza.at[layer, others_r, pl.ds(0, CH)]
+
     def place_dz(q):
         for layer in range(2):
-            wait(dza.at[layer, pl.ds(0, R - 1), pl.ds(0, CH)], dzr.at[layer, q])
+            wait(chunk_like(layer), dzr.at[layer, q])
             v = blocks_joined(lambda p: dza[layer, p, pl.ds(q * CH, CH)].astype(F32).reshape(CH * B, npad))
-            dzn_ref[layer, pl.ds(pl.multiple_of(q * (CH * B), CH * B), CH * B)] = v.astype(BF16)
+            at = pl.ds(pl.multiple_of(q * (CH * B), CH * B), CH * B)
+            dzn_ref[layer, at] = v.astype(BF16)
+            pltpu.make_async_copy(dzn_ref.at[layer, at], dzn_out.at[layer, at], outs.at[1, layer, q]).start()
 
     shift = core * ((LANE - rows % LANE) % LANE)
     per = R // 2
@@ -554,9 +581,9 @@
         @pl.when(s == 3)
         def _():
             put_left(3, jnp.concatenate([h0[r, 1].astype(F32), local_rows(hist2, T - 1)], axis=0))
-        return 0
-
-    lax.fori_loop(0, T, bwd, 0)
+            pltpu.make_async_copy(left_ref, left_out, outs.at[0, 0, 0]).start()
+
+    loop(T, bwd)
     cell_grad(0, 0, reduced(r1, 0, b1r))
     send_dz(0, 0)
 
@@ -570,12 +597,21 @@
     for k in range(1, R):
         start(gbbuf.at[r], gbbuf.at[r], gbs, gbr, row_dev(lax.rem(r + k, R)))
 
+    place_dz(0)
+    wait(gbbuf.at[others_r], gbr)
+    gb_ref[...] = blocks_joined(lambda p: gbbuf[p])
+    pltpu.make_async_copy(gb_ref, gb_out, outs.at[0, 1, 0]).start()
+    for layer in range(2):
+        for q in range(T // CH):
+            wait(chunk_like(layer), dzs.at[layer, q])
+    wait(gbbuf.at[others_r], gbs)
     wait(x_ref, sbs.at[0])
     wait(xstage, sbs.at[1])
     wait(xstage, sbs.at[2])
     for w in range(3):
-        wait(stage.at[w, pl.ds(0, R - 1)], ws.at[w])
-    wait(h0.at[pl.ds(0, R - 1)], h0s)
+        wait(stage.at[w, others_r], ws.at[w])
+    wait(h0.at[others_r], h0s)
+    wait(zh.at[others_r], zhs.at[0])
     for cut in range(len(X_CUTS) - 1):
         wait_x(cut, xss)
 
@@ -583,39 +619,44 @@
     def _():
         wait(c_in, css)
 
-    hflat = hspare.at[pl.ds(0, N - 1)]
+    hflat = hspare.at[others_n]
 
     def drain(t, _):
-        wait(r1.at[0, pl.ds(0, N - 1)], b1s.at[t])
-        wait(zs.at[pl.ds(0, CHIPS - 1), t], zss.at[t])
+        wait(r1.at[0, others_n], b1s.at[t])
+        wait(zs.at[others_c, t], zss.at[t])
         wait(hflat, h1s.at[t])
 
         @pl.when(t < T - 1)
         def _():
-            wait(r1.at[0, pl.ds(0, N - 1)], b2s.at[t])
+            wait(r1.at[0, others_n], b2s.at[t])
             wait(hflat, h2s.at[t])
-        return 0
-
-    lax.fori_loop(0, T, drain, 0)
-    place_dz(0)
-    wait(gbbuf.at[pl.ds(0, R - 1)], gbr)
-    gb_ref[...] = blocks_joined(lambda p: gbbuf[p])
+
+    loop(T, drain)
+    wait(left_ref, outs.at[0, 0, 0])
+    wait(gb_ref, outs.at[0, 1, 0])
     for layer in range(2):
         for q in range(T // CH):
-            wait(dza.at[layer, pl.ds(0, R - 1), pl.ds(0, CH)], dzs.at[layer, q])
-    wait(gbbuf.at[pl.ds(0, R - 1)], gbs)
-
-
-def grad_kernel(left_ref, dzn_ref, gb_ref, gx1, gh1, gx2, gh2, gb1, gb2, buf, sems):
+            wait(dzn_ref.at[layer, pl.ds(0, CH * B)], outs.at[1, layer, q])
+
+
+def grad_kernel(left_in, dzn_in, gb_in, gx1, gh1, gx2, gh2, gb1, gb2, left_ref, dzn_ref, gb_ref, buf, ins, sems):
     rows = gx1.shape[0]
     step = rows // GROWS
+    loads = [pltpu.make_async_copy(left_in, left_ref, ins.at[0]), pltpu.make_async_copy(dzn_in.at[1], dzn_ref.at[1], ins.at[1]),
+             pltpu.make_async_copy(dzn_in.at[0], dzn_ref.at[0], ins.at[2]), pltpu.make_async_copy(gb_in, gb_ref, ins.at[3])]
+    for load in loads:
+        load.start()
+    loads[0].wait()
     copies = []
-    for i in range(GROWS):
-        for k, (out, layer) in enumerate(((gx1, 0), (gh1, 0), (gx2, 1), (gh2, 1))):
-            lo = i * step
-            buf[k, lo:lo + step] = dot(left_ref[k, lo:lo + step], dzn_ref[layer])
-            copies.append(pltpu.make_async_copy(buf.at[k, pl.ds(lo, step)], out.at[pl.ds(lo, step)], sems.at[k, i]))
-            copies[-1].start()
+    for layer, grads in ((1, ((2, gx2), (3, gh2))), (0, ((0, gx1), (1, gh1)))):
+        loads[2 - layer].wait()
+        for i in range(GROWS):
+            for k, out in grads:
+                lo = i * step
+                buf[k, lo:lo + step] = dot(left_ref[k, lo:lo + step], dzn_ref[layer])
+                copies.append(pltpu.make_async_copy(buf.at[k, pl.ds(lo, step)], out.at[pl.ds(lo, step)], sems.at[k, i]))
+                copies[-1].start()
+    loads[3].wait()
     gb1[...] = gb_ref[0]
     gb2[...] = gb_ref[1]
     for copy in copies:
@@ -641,6 +682,7 @@
         chips = R // 2
         gw = -(-unit * R // LANE) * LANE
         vm = pl.BlockSpec(memory_space=pltpu.VMEM)
+        hbm = pl.BlockSpec(memory_space=pl.ANY)
         dma = pltpu.SemaphoreType.DMA
         V = pltpu.VMEM
         left, dzn, gb = pl.pallas_call(
@@ -649,8 +691,9 @@
             out_shape=(jax.ShapeDtypeStruct((4, npad, T * B), BF16), jax.ShapeDtypeStruct((2, T * B, cols), BF16),
                        jax.ShapeDtypeStruct((8, cols), F32)),
             in_specs=[vm] + [pl.BlockSpec(memory_space=pl.ANY)] * 4 + [vm] * 5,
-            out_specs=(vm, vm, vm),
+            out_specs=(hbm, hbm, hbm),
             scratch_shapes=[
+                V((4, npad, T * B), BF16), V((2, T * B, cols), BF16), V((8, cols), F32),
                 V((rows, cols), BF16), V((rows, cols), BF16), V((rows, cols), BF16), V((rows, cols), BF16),
                 V((B, cols), F32),
                 V((R, WIN, npad), BF16),
@@ -688,7 +731,9 @@
                 V((2, B, LANE), F32),
                 V((B, npad), BF16),
                 V((N, B, LANE), BF16),
-                dma((4,)),
+                V((R, B, npad), F32),
+                V((R, B, npad), F32),
+                dma((4,)), dma((2, 2, T // CH)), dma((2,)),
                 dma((3,)), dma((3,)), dma((3,)), dma((3,)), dma((len(X_CUTS) - 1,)), dma((len(X_CUTS) - 1,)), dma((T,)), dma((T,)),
                 dma, dma, dma, dma,
                 dma((T,)), dma((T, C)), dma((T,)), dma((T, C)),
@@ -700,15 +745,15 @@
 
         out = jax.ShapeDtypeStruct((rows, cols), F32)
         bout = jax.ShapeDtypeStruct((cols,), F32)
-        hbm = pl.BlockSpec(memory_space=pl.ANY)
         return tuple(pl.pallas_call(
             grad_kernel,
             name='grads',
             out_shape=(out,) * 4 + (bout,) * 2,
-            in_specs=[vm] * 3,
+            in_specs=[hbm] * 3,
             out_specs=(hbm,) * 4 + (vm,) * 2,
-            scratch_shapes=[V((4, rows, cols), F32), dma((4, GROWS))],
-            compiler_params=pltpu.CompilerParams(vmem_limit_bytes=40 * 1024 * 1024),
+            scratch_shapes=[V((4, npad, T * B), BF16), V((2, T * B, cols), BF16), V((8, cols), F32),
+                            V((4, rows, cols), F32), dma((4,)), dma((4, GROWS))],
+            compiler_params=pltpu.CompilerParams(vmem_limit_bytes=63 * 1024 * 1024),
         )(left, dzn, gb))
 
     return jax.shard_map(local_grads, mesh=mesh,

time: 260 us -> 254 us (0.977)
  local copies, waits for them, and re-layouts: 3.24 us -> 0 us
  Pallas kernels: 256 us -> 253 us
    pallas_call x1, Pallas kernels: 249 us -> 245 us  [local_grads(): pl.pallas_call(functools.partial(recur_kernel, C, R, T, B, U), name='recu...]
    unnamed x6 -> x0, local copies, waits for them, and re-layouts: 3.24 us -> none
where the time goes in v3:
time: 254 us
  Pallas kernels  253 us (100%)
    pallas_call x1, Pallas kernels, local_grads(): pl.pallas_call(functools.partial(recur_kernel, C, R, T, B, U), name='recu...  245 us
    pallas_call x1, Pallas kernels, local_grads(): pl.pallas_call(grad_kernel, name='grads', out_shape=(out,) * 4 + (bout,)...  7.88 us

profile of v3, /device:TPU:97, one launch (start us, length us, event | category | flops | bytes accessed | tf_op | source)
XLA Modules:
  0.0 254.0 jit_solution(9401017695285493620)
XLA Ops:
  0.6 245.3 %recur.1 = (bf16[4,384,128]{2,1,0:T(8,128)(2,1)}, bf16[2,128,2816]{2,1,0:T(8,128)(2,1)}, f32[8,2816]{1,0:T(8,128)}) custom-call(bf16[16,8,352]{2,1,0:T(8,128)(2,1)} %x_ref.1, bf16[352,2816]{1,0:T(8,128)(2,1)} %wx1_ref.1, bf16[352,2816]{1,0:T(8,128)(2,1)} %wh1_ref.1, bf16[352,2816]{1,0:T(8,128)(2,1)} %wx2_ref.1, bf16[352,2816]{1,0:T(8,128)(2,1)} %wh2_ref.1, ...), custom_call_target="tpu_custom_call" | custom-call | tf_op jit(solution)/shard_map/recur/pallas_call | solution.py:688
  245.9 7.9 %grads.1 = (f32[352,2816]{1,0:T(8,128)}, f32[352,2816]{1,0:T(8,128)}, f32[352,2816]{1,0:T(8,128)}, f32[352,2816]{1,0:T(8,128)}, f32[2816]{0:T(1024)}, /*index=5*/f32[2816]{0:T(1024)}) custom-call(bf16[4,384,128]{2,1,0:T(8,128)(2,1)} %get-tuple-element.9.left_in, bf16[2,128,2816]{2,1,0:T(8,128)(2,1)} %get-tuple-element.10.dzn_in, ...), custom_call_target="tpu_custom_call" | custom-call | tf_op jit(solution)/shard_map/grads/pallas_call | solution.py:748

commit v4 on v3

--- a/solution.py
+++ b/solution.py
@@ -509,8 +509,8 @@
     def chunk_like(layer):
         return dza.at[layer, others_r, pl.ds(0, CH)]
 
-    def place_dz(q):
-        for layer in range(2):
+    def place_dz(q, layers=(1, 0)):
+        for layer in layers:
             wait(chunk_like(layer), dzr.at[layer, q])
             v = blocks_joined(lambda p: dza[layer, p, pl.ds(q * CH, CH)].astype(F32).reshape(CH * B, npad))
             at = pl.ds(pl.multiple_of(q * (CH * B), CH * B), CH * B)
@@ -584,6 +584,7 @@
             pltpu.make_async_copy(left_ref, left_out, outs.at[0, 0, 0]).start()
 
     loop(T, bwd)
+    place_dz(0, (1,))
     cell_grad(0, 0, reduced(r1, 0, b1r))
     send_dz(0, 0)
 
@@ -597,7 +598,7 @@
     for k in range(1, R):
         start(gbbuf.at[r], gbbuf.at[r], gbs, gbr, row_dev(lax.rem(r + k, R)))
 
-    place_dz(0)
+    place_dz(0, (0,))
     wait(gbbuf.at[others_r], gbr)
     gb_ref[...] = blocks_joined(lambda p: gbbuf[p])
     pltpu.make_async_copy(gb_ref, gb_out, outs.at[0, 1, 0]).start()

time: 254 us -> 254 us (level)
  no operation moved by 1% of the time
where the time goes in v4:
time: 254 us
  Pallas kernels  253 us (100%)
    pallas_call x1, Pallas kernels, local_grads(): pl.pallas_call(functools.partial(recur_kernel, C, R, T, B, U), name='recu...  245 us
    pallas_call x1, Pallas kernels, local_grads(): pl.pallas_call(grad_kernel, name='grads', out_shape=(out,) * 4 + (bout,)...  7.88 us

profile of v4, /device:TPU:97, one launch (start us, length us, event | category | flops | bytes accessed | tf_op | source)
XLA Modules:
  0.0 254.0 jit_solution(3002958115057393702)
XLA Ops:
  0.6 245.3 %recur.1 = (bf16[4,384,128]{2,1,0:T(8,128)(2,1)}, bf16[2,128,2816]{2,1,0:T(8,128)(2,1)}, f32[8,2816]{1,0:T(8,128)}) custom-call(bf16[16,8,352]{2,1,0:T(8,128)(2,1)} %x_ref.1, bf16[352,2816]{1,0:T(8,128)(2,1)} %wx1_ref.1, bf16[352,2816]{1,0:T(8,128)(2,1)} %wh1_ref.1, bf16[352,2816]{1,0:T(8,128)(2,1)} %wx2_ref.1, bf16[352,2816]{1,0:T(8,128)(2,1)} %wh2_ref.1, ...), custom_call_target="tpu_custom_call" | custom-call | tf_op jit(solution)/shard_map/recur/pallas_call | solution.py:689
  245.9 7.9 %grads.1 = (f32[352,2816]{1,0:T(8,128)}, f32[352,2816]{1,0:T(8,128)}, f32[352,2816]{1,0:T(8,128)}, f32[352,2816]{1,0:T(8,128)}, f32[2816]{0:T(1024)}, /*index=5*/f32[2816]{0:T(1024)}) custom-call(bf16[4,384,128]{2,1,0:T(8,128)(2,1)} %get-tuple-element.9.left_in, bf16[2,128,2816]{2,1,0:T(8,128)(2,1)} %get-tuple-element.10.dzn_in, ...), custom_call_target="tpu_custom_call" | custom-call | tf_op jit(solution)/shard_map/grads/pallas_call | solution.py:749
